TPU v7x, 32 devices: a whole 2x2x4 slice. The times are simulated.
32 devices in a mesh: image: 8 (over z, x), space: 4 (over y, core).
Axes of the slice: x: 2, y: 2, z: 4, core: 2. Of those that a mesh axis runs over, the one named last changes fastest.
Arguments:
- magnet: float32 [16, 3, 8, 256, 256], P('image', None, None, 'space'), may hold values from -1 to 1, as said below
- anisotropy: float32 [256], P('space'), may hold values from 0.25 to 10
- kernel: float32 [6, 16, 512, 512], P(None, 'space'), as said below
Outputs:
- updated_magnet: float32 [16, 3, 8, 256, 256], P('image', None, None, 'space')
- band_force: float32 [16, 3, 8, 256, 256], P('image', None, None, 'space')
- energy: float32 [16], P('image')
Inputs may be any that keep to these rules, and one draw needn't show every extreme that they name: `magnet`: each cell's three components form a unit vector. `kernel`: each component is even under k -> -k modulo the padded length along every frequency index, except that xy is odd along x and y, xz odd along x and z, and yz odd along y and z.
All inputs are finite; a program needn't handle non-finite values.
Results may differ from a plain program's by a relative error of at most 0.0003.
Values sent between devices are 32-bit elements; how exact they have to be, the bound alone decides.
A program may use at most 256 MiB of HBM per device.

v0:
```python
import math

import jax
import jax.numpy as jnp
from jax import lax
from jax.sharding import PartitionSpec as P

exchange_strength = 0.25
chiral_strength = 0.3
spring_strength = 10.0
step_limit = 1.0
rotation_limit = 0.5
epsilon = 1e-06


def extended(cells, sides, width):
    for axis, dim in sides:
        count = lax.axis_size(axis)
        ends = count - 1
        head = lax.slice_in_dim(cells, 0, width, axis=dim)
        tail = lax.slice_in_dim(cells, cells.shape[dim] - width, cells.shape[dim], axis=dim)
        cells = jnp.concatenate(
            [
                lax.ppermute(tail, axis, [(i, (i + 1) % count) for i in range(ends)]),
                cells,
                lax.ppermute(head, axis, [((i + 1) % count, i) for i in range(ends)]),
            ],
            axis=dim,
        )
    return cells


def lift_axes(values):
    return values[:, None, None, None, None]


def total_cells(values):
    return jnp.sum(values, axis=tuple(range(1, values.ndim)))


def project(vector, magnet):
    return vector - jnp.sum(vector * magnet, axis=1, keepdims=True) * magnet


def angle_squared(first, second):
    normal_part = jnp.cross(first, second, axis=1)
    sine_value = jnp.sqrt(jnp.sum(normal_part * normal_part, axis=1))
    cosine = jnp.sum(first * second, axis=1)
    return jnp.arctan2(sine_value, cosine) ** 2


def tangent_weights(energy_total, energy_next, energy_prior):
    rise_next = energy_next - energy_total
    rise_prior = energy_total - energy_prior
    upward = (rise_next > 0) & (rise_prior > 0)
    downward = (rise_next < 0) & (rise_prior < 0)
    larger = jnp.maximum(jnp.abs(rise_next), jnp.abs(rise_prior))
    smaller = jnp.minimum(jnp.abs(rise_next), jnp.abs(rise_prior))
    toward_next = energy_next > energy_prior
    weight_next = jnp.where(
        upward, 1.0, jnp.where(downward, 0.0, jnp.where(toward_next, larger, smaller))
    )
    weight_prior = jnp.where(
        upward, 0.0, jnp.where(downward, 1.0, jnp.where(toward_next, smaller, larger))
    )
    return (weight_next, weight_prior)


def phase_pair(count_in, count_out, length, flipped):
    row_index = lax.broadcasted_iota(jnp.int32, (count_in, count_out), 0)
    column_index = lax.broadcasted_iota(jnp.int32, (count_in, count_out), 1)
    phase_angle = (row_index * column_index % length).astype(jnp.float32) * (2.0 * math.pi / length)
    return (jnp.cos(phase_angle), flipped * jnp.sin(phase_angle))


def real_table(count_in, count_out, length):
    cosine, sine_value = phase_pair(count_in, count_out, length, -1.0)
    return jnp.stack([cosine, sine_value])


def complex_table(count_in, count_out, length, flipped):
    cosine, sine_value = phase_pair(count_in, count_out, length, flipped)
    upper_block = jnp.stack([cosine, sine_value])
    lower_block = jnp.stack([-sine_value, cosine])
    return jnp.stack([upper_block, lower_block])


def real_part_table(count_in, count_out, length):
    cosine, sine_value = phase_pair(count_in, count_out, length, 1.0)
    return jnp.stack([cosine, -sine_value])


def contract(pattern, left, right):
    return jnp.einsum(
        pattern, left, right, precision=lax.Precision.HIGHEST, preferred_element_type=jnp.float32
    )


def demag_field(magnet, kernel):
    layer_count = magnet.shape[2]
    column_count = magnet.shape[4]
    full_rows = kernel.shape[2] // 2
    across = contract(
        "bczxy,szq->bcqsxy", magnet, real_table(layer_count, 2 * layer_count, 2 * layer_count)
    )
    planes = lax.all_to_all(across, "space", split_axis=2, concat_axis=4, tiled=True)
    planes = contract(
        "bcqrxy,rsyv->bcqsxv",
        planes,
        complex_table(column_count, 2 * column_count, 2 * column_count, -1.0),
    )
    spectrum = contract(
        "bcqrxv,rsxu->bcqsuv", planes, complex_table(full_rows, 2 * full_rows, 2 * full_rows, -1.0)
    )
    spec_x = spectrum[:, 0]
    spec_y = spectrum[:, 1]
    spec_z = spectrum[:, 2]
    field_x = (
        kernel[0][:, None] * spec_x + kernel[3][:, None] * spec_y + kernel[4][:, None] * spec_z
    )
    field_y = (
        kernel[3][:, None] * spec_x + kernel[1][:, None] * spec_y + kernel[5][:, None] * spec_z
    )
    field_z = (
        kernel[4][:, None] * spec_x + kernel[5][:, None] * spec_y + kernel[2][:, None] * spec_z
    )
    response = jnp.stack([field_x, field_y, field_z], axis=1)
    response = contract(
        "bcqrxv,rsxu->bcqsuv", response, complex_table(2 * full_rows, full_rows, 2 * full_rows, 1.0)
    )
    response = contract(
        "bcqrxv,rsvy->bcqsxy",
        response,
        complex_table(2 * column_count, column_count, 2 * column_count, 1.0),
    )
    returned = lax.all_to_all(response, "space", split_axis=4, concat_axis=2, tiled=True)
    result = contract(
        "bcqsxy,sqz->bczxy",
        returned,
        real_part_table(2 * layer_count, layer_count, 2 * layer_count),
    )
    padded_cells = 8 * layer_count * full_rows * column_count
    return result * (-1.0 / padded_cells)


def local_fields(magnet, anisotropy, kernel):
    layer_count = magnet.shape[2]
    row_count = magnet.shape[3]
    column_count = magnet.shape[4]
    rimmed = extended(magnet, (("space", 3),), 1)
    x_plus = rimmed[:, :, :, 2:]
    x_minus = rimmed[:, :, :, :-2]
    padded = jnp.pad(magnet, ((0, 0), (0, 0), (1, 1), (0, 0), (1, 1)))
    z_plus = padded[:, :, 2:, :, 1:-1]
    z_minus = padded[:, :, :-2, :, 1:-1]
    y_plus = padded[:, :, 1:-1, :, 2:]
    y_minus = padded[:, :, 1:-1, :, :-2]
    first_row = lax.axis_index("space") * row_count
    full_rows = row_count * lax.axis_size("space")
    layer_pos = lax.broadcasted_iota(jnp.int32, (layer_count, row_count, column_count), 0)
    row_pos = lax.broadcasted_iota(jnp.int32, (layer_count, row_count, column_count), 1) + first_row
    column_pos = lax.broadcasted_iota(jnp.int32, (layer_count, row_count, column_count), 2)
    boundary = (layer_pos == 0).astype(jnp.float32) + (layer_pos == layer_count - 1).astype(
        jnp.float32
    )
    boundary = (
        boundary
        + (row_pos == 0).astype(jnp.float32)
        + (row_pos == full_rows - 1).astype(jnp.float32)
    )
    boundary = (
        boundary
        + (column_pos == 0).astype(jnp.float32)
        + (column_pos == column_count - 1).astype(jnp.float32)
    )
    present = 6.0 - boundary
    neighbours = x_plus + x_minus + y_plus + y_minus + z_plus + z_minus
    exchange_part = exchange_strength * (neighbours - present * magnet)
    chiral_x = chiral_strength * (x_plus[:, 2] - x_minus[:, 2])
    chiral_y = chiral_strength * (y_plus[:, 2] - y_minus[:, 2])
    chiral_z = -chiral_strength * (x_plus[:, 0] - x_minus[:, 0] + (y_plus[:, 1] - y_minus[:, 1]))
    easy_axis = 2.0 * anisotropy[:, None] * magnet[:, 2]
    local_part = exchange_part + jnp.stack([chiral_x, chiral_y, chiral_z + easy_axis], axis=1)
    return local_part + demag_field(magnet, kernel)


def body(magnet, anisotropy, kernel):
    image_count = magnet.shape[0]
    cell_count = magnet.shape[2] * magnet.shape[3] * lax.axis_size("space") * magnet.shape[4]
    fields = local_fields(magnet, anisotropy, kernel)
    framed = extended(magnet, (("image", 0),), 1)
    prior_image = framed[:-2]
    next_image = framed[2:]
    true_force = project(fields, magnet)
    tangent_next = project(next_image - magnet, magnet)
    tangent_prior = project(magnet - prior_image, magnet)
    energy_part = -0.5 * total_cells(magnet * fields)
    next_part = total_cells(angle_squared(magnet, next_image))
    prior_part = total_cells(angle_squared(magnet, prior_image))
    energy_total, next_squares, prior_squares = lax.psum(
        (energy_part, next_part, prior_part), "space"
    )
    framed_energy = extended(energy_total, (("image", 0),), 1)
    weight_next, weight_prior = tangent_weights(energy_total, framed_energy[2:], framed_energy[:-2])
    tangent = lift_axes(weight_next) * tangent_next + lift_axes(weight_prior) * tangent_prior
    length_squares, drive_total = lax.psum(
        (total_cells(tangent * tangent), total_cells(true_force * tangent)), "space"
    )
    tangent_scale = jnp.sqrt(length_squares / cell_count + epsilon)
    unit_tangent = tangent / lift_axes(tangent_scale)
    parallel = drive_total / (cell_count * tangent_scale)
    distance_next = jnp.sqrt(next_squares / cell_count)
    distance_prior = jnp.sqrt(prior_squares / cell_count)
    spring = spring_strength * (distance_next - distance_prior)
    image_index = lax.axis_index("image") * image_count + jnp.arange(image_count)
    band_size = image_count * lax.axis_size("image")
    interior = (image_index > 0) & (image_index < band_size - 1)
    band_force = jnp.where(
        lift_axes(interior), true_force + lift_axes(spring - parallel) * unit_tangent, 0.0
    )
    local_largest = jnp.max(jnp.sqrt(jnp.sum(band_force * band_force, axis=1)), axis=(1, 2, 3))
    largest = lax.pmax(local_largest, "space")
    move_scale = jnp.minimum(step_limit, rotation_limit / (largest + epsilon))
    stepped = magnet + lift_axes(move_scale) * band_force
    updated = stepped / jnp.sqrt(jnp.sum(stepped * stepped, axis=1, keepdims=True))
    return (updated, band_force, energy_total / cell_count)


def solution(mesh):
    in_specs = (P("image", None, None, "space", None), P("space"), P(None, "space", None, None))
    out_specs = (
        P("image", None, None, "space", None),
        P("image", None, None, "space", None),
        P("image"),
    )
    return jax.shard_map(body, mesh=mesh, in_specs=in_specs, out_specs=out_specs, check_vma=False)
```

profile of v0, /device:TPU:0, one launch (start us, length us, event | category | flops | bytes accessed | tf_op | source)
XLA Modules:
  0.0 804.6 jit_solution(16947918537953253900)
XLA Ops:
  0.6 0.1 sine_multiply_fusion.1
  0.7 14.5 %convolution_bitcast_fusion = f32[2,3,16,2,64,256]{5,2,4,1,0,3:T(8,128)} fusion(f32[1,8,16]{2,1,0:T(8,128)S(1)} %get-tuple-element.75, f32[1,8,16]{2,1,0:T(8,128)S(1)} %get-tuple-element.76, f32[2,3,8,64,256]{4,3,2,1,0:T(8,128)} %param.5), kind=kOutput, calls=%fused_computation.20 | convolution fusion | flops 301990144 | bytes 15729664 | tf_op jit(solution)/shard_map/bczxy,szq->bcqsxy/dot_general | solution.py:94
  15.2 16.3 %copy.143 = f32[2,3,16,2,64,256]{5,4,1,0,3,2:T(8,128)} copy(f32[2,3,16,2,64,256]{5,2,4,1,0,3:T(8,128)} %convolution_bitcast_fusion) | data formatting | bytes 25165824 | tf_op jit(solution)/shard_map/bczxy,szq->bcqsxy/transpose | solution.py:94
  31.5 6.5 all-to-all-start
  38.0 1.9 fusion.76
  40.0 1.9 fusion.77
  41.9 2.1 fusion.74
  44.0 2.1 sine_multiply_fusion
  46.0 1.6 maximum_bitcast_fusion.3
  47.6 0.2 maximum_bitcast_fusion.5
  47.8 17.2 %slice_bitcast_fusion.5 = (f32[4,512,512]{2,1,0:T(8,128)}, f32[4,512,512]{2,1,0:T(8,128)}, f32[4,512,512]{2,1,0:T(8,128)}, f32[4,512,512]{2,1,0:T(8,128)}, f32[4,512,512]{2,1,0:T(8,128)}, /*index=5*/f32[4,512,512]{2,1,0:T(8,128)}) fusion(f32[6,4,512,512]{3,2,1,0:T(8,128)} %param.7), kind=kLoop, calls=%fused_computation.26 | loop fusion | bytes 50331648 | tf_op jit(solution)/shard_map/mul | solution.py:119
  65.0 111.7 %all-to-all-done = f32[2,3,16,2,64,256]{5,4,1,0,3,2:T(8,128)} async-done(((f32[2,3,16,2,64,256]{5,4,1,0,3,2:T(8,128)}), f32[2,3,16,2,64,256]{5,4,1,0,3,2:T(8,128)}, u32[]{:S(2)}, u32[]{:S(2)}) %all-to-all-start) | async-done | bytes 12582944 | tf_op jit(solution)/shard_map/all_to_all | solution.py:106
  176.8 11.2 %copy.145 = f32[2,3,4,2,4,64,256]{6,5,4,3,2,1,0:T(8,128)} copy(f32[2,3,4,2,4,64,256]{6,5,1,0,3,2,4:T(8,128)} %bitcast.21) | data formatting | bytes 25165824 | tf_op jit(solution)/shard_map/all_to_all | solution.py:106
  188.0 45.6 %fusion.42 = f32[2,512,2,3,4,256,1]{5,1,6,0,4,3,2:T(8,128)} fusion(f32[2,3,4,2,256,256,1]{5,4,3,6,2,1,0:T(8,128)} %bitcast.209, f32[1,2,256,512]{2,3,0,1:T(8,128)S(1)} %get-tuple-element.64, f32[1,2,256,512]{2,3,0,1:T(8,128)S(1)} %get-tuple-element.63), kind=kOutput, calls=%fused_computation.73 | convolution fusion | flops 38655229952 | bytes 39845888 | tf_op jit(solution)/shard_map/bcqrxy,rsyv->bcqsxv/dot_general | solution.py:94
  233.6 86.9 %fusion.6 = f32[2,3,4,2,512,512]{5,4,2,1,0,3:T(8,128)} fusion(f32[2,512,2,3,4,256,1]{5,1,6,0,4,3,2:T(8,128)} %fusion.42, f32[1,2,256,512]{2,3,0,1:T(8,128)S(1)} %get-tuple-element.64, f32[1,2,256,512]{2,3,0,1:T(8,128)S(1)} %get-tuple-element.63), kind=kOutput, calls=%fused_computation.15 | convolution fusion | flops 77309935616 | bytes 77594624 | tf_op jit(solution)/shard_map/bcqrxv,rsxu->bcqsuv/dot_general | solution.py:94
  320.5 0.0 copy-start.6
  320.5 42.9 %multiply_add_fusion.2 = (f32[2,1,4,2,512,512]{5,4,2,1,0,3:T(8,128)}, f32[2,1,4,2,512,512]{5,4,2,1,0,3:T(8,128)}, f32[2,1,4,2,512,512]{5,4,2,1,0,3:T(8,128)}) fusion(f32[2,3,4,2,512,512]{5,4,2,1,0,3:T(8,128)} %fusion.6, f32[4,512,512]{2,1,0:T(8,128)} %get-tuple-element.38, f32[4,512,512]{2,1,0:T(8,128)} %get-tuple-element.39, ...), kind=kLoop, calls=%fused_computation.18 | loop fusion | flops 62914560 | bytes 125829120 | tf_op jit(solution)/shard_map/add | solution.py:119
  363.4 86.1 %fusion = f32[2,256,2,3,4,512,1]{5,1,6,0,4,3,2:T(8,128)} fusion(f32[1,2,512,256]{2,3,0,1:T(8,128)S(1)} %copy-done.7, f32[1,2,512,256]{2,3,0,1:T(8,128)S(1)} %copy-done.6, f32[2,1,4,2,512,512]{5,4,2,1,0,3:T(8,128)} %get-tuple-element.35, f32[2,1,4,2,512,512]{5,4,2,1,0,3:T(8,128)} %get-tuple-element.34, f32[2,1,4,2,512,512]{5,4,2,1,0,3:T(8,128)} %get-tuple-element.33), kind=kOutput, calls=%fused_computation.1 | convolution fusion | flops 77335101440 | bytes 77594624 | tf_op jit(solution)/shard_map/bcqrxv,rsxu->bcqsuv/dot_general | solution.py:94
  449.5 46.3 %fusion.9 = f32[2,3,4,2,256,256]{4,5,2,1,0,3:T(8,128)} fusion(f32[2,256,2,3,4,512,1]{5,1,6,0,4,3,2:T(8,128)} %fusion, f32[1,2,512,256]{2,3,0,1:T(8,128)S(1)} %copy-done.7, f32[1,2,512,256]{2,3,0,1:T(8,128)S(1)} %copy-done.6), kind=kOutput, calls=%fused_computation.19 | convolution fusion | flops 38655229952 | bytes 39845888 | tf_op jit(solution)/shard_map/bcqrxv,rsvy->bcqsxy/dot_general | solution.py:94
  495.8 15.4 %copy.148 = f32[2,3,4,2,256,256]{5,2,1,0,3,4:T(4,128)} copy(f32[2,3,4,2,256,256]{4,5,2,1,0,3:T(8,128)} %fusion.9) | data formatting | bytes 25165824 | tf_op jit(solution)/shard_map/bcqrxv,rsvy->bcqsxy/transpose | solution.py:94
  511.2 6.8 all-to-all-start.1
  518.0 1.8 copy.177
  519.8 0.0 copy-start.1
  519.8 2.4 collective-permute-start.1
  522.2 1.3 collective-permute-start
  523.5 2.1 fusion.105
  525.7 1.3 collective-permute-start.2
  527.0 6.0 collective-permute-start.3
  533.0 0.1 sine_negate_fusion
  533.1 1.0 add_subtract_fusion
  534.1 1.8 copy.221
  536.0 1.8 constant_dynamic-update-slice_fusion.1
  537.9 3.3 fusion.53
  541.2 0.2 copy-done.4
  541.4 22.5 %collective-permute-done.2 = f32[1,3,8,64,256]{4,2,3,1,0:T(8,128)} collective-permute-done((f32[1,3,8,64,256]{4,2,3,1,0:T(8,128)}, f32[1,3,8,64,256]{4,2,3,1,0:T(8,128)}, u32[]{:S(2)}, u32[]{:S(2)}) %collective-permute-start.2) | collective-permute-done | bytes 1572896 | tf_op jit(solution)/shard_map/ppermute | solution.py:26
  563.9 35.6 %collective-permute-done.3 = f32[1,3,8,64,256]{4,2,3,1,0:T(8,128)} collective-permute-done((f32[1,3,8,64,256]{4,2,3,1,0:T(8,128)}, f32[1,3,8,64,256]{4,2,3,1,0:T(8,128)}, u32[]{:S(2)}, u32[]{:S(2)}) %collective-permute-start.3) | collective-permute-done | bytes 1572896 | tf_op jit(solution)/shard_map/ppermute | solution.py:24
  599.5 6.1 fusion.36
  605.6 0.4 fusion.58
  606.0 0.6 subtract_bitcast_fusion.1
  606.6 1.2 fusion.40
  607.8 1.2 fusion.38
  609.1 47.0 %all-to-all-done.1 = f32[2,3,4,2,256,256]{5,2,1,0,3,4:T(4,128)} async-done(((f32[2,3,4,2,256,256]{5,2,1,0,3,4:T(4,128)}), f32[2,3,4,2,256,256]{5,2,1,0,3,4:T(4,128)}, u32[]{:S(2)}, u32[]{:S(2)}) %all-to-all-start.1) | async-done | bytes 12582944 | tf_op jit(solution)/shard_map/all_to_all | solution.py:136
  656.1 16.3 %copy.149 = f32[2,3,4,2,256,256]{5,4,3,2,1,0:T(8,128)} copy(f32[2,3,4,2,256,256]{5,2,1,0,3,4:T(4,128)} %all-to-all-done.1) | data formatting | bytes 25165824 | tf_op jit(solution)/shard_map/all_to_all | solution.py:136
  672.4 16.5 %copy.150 = f32[2,3,4,4,2,64,256]{6,3,2,4,5,1,0:T(4,128)} copy(f32[2,3,4,4,2,64,256]{6,5,2,4,3,1,0:T(8,128)} %bitcast.210) | data formatting | bytes 25165824 | tf_op jit(solution)/shard_map/all_to_all | solution.py:136
  688.9 14.7 %all_to_all.33 = f32[2,3,16,2,64,256]{5,2,3,4,1,0:T(8,128)} reshape(f32[2,3,4,4,2,64,256]{6,3,2,4,5,1,0:T(4,128)} %copy.150) | data formatting | bytes 25165824 | tf_op jit(solution)/shard_map/all_to_all | solution.py:136
  703.6 20.7 %multiply_reduce_fusion.5 = (f32[2,8,64,256]{3,1,2,0:T(8,128)}, f32[2]{0:T(128)S(1)}, f32[2,3,8,64,256]{4,2,3,1,0:T(8,128)}) fusion(f32[2,3,8,64,256]{4,3,2,1,0:T(8,128)S(1)} %copy-done, f32[2,3,16,2,64,256]{5,2,3,4,1,0:T(8,128)} %all_to_all.33, f32[1,16,8]{1,2,0:T(8,128)S(1)} %get-tuple-element.85, f32[1,16,8]{1,2,0:T(8,128)S(1)} %get-tuple-element.86, ...), kind=kOutput, calls=%fused_computation.80 | convolution fusion | flops 314310912 | bytes 33031176 | tf_op jit(solution)/shard_map/bcqsxy,sqz->bczxy/dot_general | solution.py:94
  724.3 5.9 multiply_reduce_fusion.6
  730.3 19.4 %psum.37 = f32[2]{0:T(128)S(1)} all-reduce(f32[2]{0:T(128)S(1)} %broadcast_multiply_fusion), channel_id=1, replica_groups=mesh['image'=8,'space'=4] {'space'}, use_global_device_ids=true, to_apply=%region_10.12 | all-reduce | flops 2 | bytes 16 | tf_op jit(solution)/shard_map/psum | solution.py:200
  749.6 0.7 fusion.107
  750.3 1.5 collective-permute-start.4
  751.8 5.4 collective-permute-start.5
  757.2 0.8 collective-permute-done.5
  758.0 1.3 pad_maximum_fusion.8
  759.3 0.5 select_select_fusion.1
  759.8 10.0 %multiply_reduce_fusion.3 = (f32[2]{0:T(128)S(1)}, f32[2]{0:T(128)S(1)}, f32[2,3,8,64,256]{4,2,3,1,0:T(8,128)}) fusion(f32[2,3,8,64,256]{4,2,3,1,0:T(8,128)} %get-tuple-element.74, f32[2,8,64,256]{3,1,2,0:T(8,128)} %get-tuple-element.16, f32[2,3,8,64,256]{4,3,2,1,0:T(8,128)S(1)} %copy-done, f32[2,3,8,64,256]{4,2,3,1,0:T(8,128)} %copy-done.1, ...), kind=kLoop, calls=%fused_computation.69 | loop fusion | flops 13369340 | bytes 18874400 | tf_op jit(solution)/shard_map/reduce_sum | solution.py:38
  769.8 6.5 all-reduce.1
  776.3 8.2 %multiply_reduce_fusion.1 = (f32[2,8,64,256]{3,1,2,0:T(8,128)S(1)}, f32[2,3,8,64,256]{4,2,3,1,0:T(8,128)}) fusion(f32[2,3,8,64,256]{4,2,3,1,0:T(8,128)} %get-tuple-element.32, f32[2]{0:T(128)S(1)} %get-tuple-element.69, f32[2]{0:T(128)S(1)} %get-tuple-element.68, f32[2,3,8,64,256]{4,2,3,1,0:T(8,128)} %get-tuple-element.74, ...), kind=kLoop, calls=%fused_computation.66 | loop fusion | flops 6029312 | bytes 14680082 | tf_op jit(solution)/shard_map/reduce_sum | solution.py:221
  784.5 0.4 sqrt_reduce_fusion
  784.9 6.7 pmax.7
  791.6 4.7 copy.179
  796.3 2.8 multiply_reduce_fusion
  799.1 0.2 sqrt.32
  799.3 2.2 broadcast_divide_fusion
  801.5 2.6 copy.178
  (29 shorter events, 0.1 us)
Async XLA Ops:
  31.5 145.3 %all-to-all-start = ((f32[2,3,16,2,64,256]{5,4,1,0,3,2:T(8,128)}), f32[2,3,16,2,64,256]{5,4,1,0,3,2:T(8,128)}, u32[]{:S(2)}, u32[]{:S(2)}) async-start(f32[2,3,16,2,64,256]{5,4,1,0,3,2:T(8,128)} %copy.143), calls=%async_computation | async-start | bytes 25165824 | tf_op jit(solution)/shard_map/all_to_all | solution.py:106
  320.5 42.9 %copy-start.6 = (f32[1,2,512,256]{2,3,0,1:T(8,128)S(1)}, f32[1,2,512,256]{2,3,0,1:T(8,128)}, u32[]{:S(2)}) copy-start(f32[1,2,512,256]{2,3,0,1:T(8,128)} %get-tuple-element.61) | copy-start | bytes 3145732
  320.5 42.9 %copy-start.7 = (f32[1,2,512,256]{2,3,0,1:T(8,128)S(1)}, f32[1,2,512,256]{2,3,0,1:T(8,128)}, u32[]{:S(2)}) copy-start(f32[1,2,512,256]{2,3,0,1:T(8,128)} %get-tuple-element.62) | copy-start | bytes 3145732
  511.2 6.8 copy-start
  511.2 144.9 %all-to-all-start.1 = ((f32[2,3,4,2,256,256]{5,2,1,0,3,4:T(4,128)}), f32[2,3,4,2,256,256]{5,2,1,0,3,4:T(4,128)}, u32[]{:S(2)}, u32[]{:S(2)}) async-start(f32[2,3,4,2,256,256]{5,2,1,0,3,4:T(4,128)} %copy.148), calls=%async_computation.1 | async-start | bytes 25165824 | tf_op jit(solution)/shard_map/all_to_all | solution.py:136
  519.8 5.9 copy-start.1
  519.8 16.1 %collective-permute-start.1 = (f32[2,3,8,1,256]{4,2,3,1,0:T(8,128)S(1)}, f32[2,3,8,1,256]{4,2,3,1,0:T(8,128)S(1)}, u32[]{:S(2)}, u32[]{:S(2)}) collective-permute-start(f32[2,3,8,1,256]{4,2,3,1,0:T(8,128)S(1)} %get-tuple-element.58), channel_id=1, source_target_pairs={{0,1},{1,2},{2,3},{4,5},{5,6},{6,7},{8,9},{9,10},{10,11},{12,13},{... | collective-permute-start | bytes 147464 | tf_op jit(solution)/shard_map/ppermute | solution.py:24
  522.2 10.8 %copy-start.8 = (f32[64]{0:T(128)S(1)}, f32[64]{0:T(128)}, u32[]{:S(2)}) copy-start(f32[64]{0:T(128)} %param.6) | copy-start | bytes 772
  522.2 15.6 %collective-permute-start = (f32[2,3,8,1,256]{4,2,3,1,0:T(8,128)S(1)}, f32[2,3,8,1,256]{4,2,3,1,0:T(8,128)S(1)}, u32[]{:S(2)}, u32[]{:S(2)}) collective-permute-start(f32[2,3,8,1,256]{4,2,3,1,0:T(8,128)S(1)} %get-tuple-element.57), channel_id=1, source_target_pairs={{1,0},{2,1},{3,2},{5,4},{6,5},{7,6},{9,8},{10,9},{11,10},{13,12},{... | collective-permute-start | bytes 147464 | tf_op jit(solution)/shard_map/ppermute | solution.py:26
  525.7 38.2 %collective-permute-start.2 = (f32[1,3,8,64,256]{4,2,3,1,0:T(8,128)}, f32[1,3,8,64,256]{4,2,3,1,0:T(8,128)}, u32[]{:S(2)}, u32[]{:S(2)}) collective-permute-start(f32[1,3,8,64,256]{4,2,3,1,0:T(8,128)} %get-tuple-element.56), channel_id=1, source_target_pairs={{4,0},{8,4},{12,8},{16,12},{20,16},{24,20},{28,24},{5,1},{9,5},{13... | collective-permute-start | bytes 4718600 | tf_op jit(solution)/shard_map/ppermute | solution.py:26
  527.0 72.5 %collective-permute-start.3 = (f32[1,3,8,64,256]{4,2,3,1,0:T(8,128)}, f32[1,3,8,64,256]{4,2,3,1,0:T(8,128)}, u32[]{:S(2)}, u32[]{:S(2)}) collective-permute-start(f32[1,3,8,64,256]{4,2,3,1,0:T(8,128)} %get-tuple-element.55), channel_id=1, source_target_pairs={{0,4},{4,8},{8,12},{12,16},{16,20},{20,24},{24,28},{1,5},{5,9},{9,... | collective-permute-start | bytes 4718600 | tf_op jit(solution)/shard_map/ppermute | solution.py:24
  536.0 1.9 copy-start.2
  537.8 3.4 copy-start.5
  537.9 3.6 copy-start.4
  750.3 6.9 collective-permute-start.4
  751.8 6.2 collective-permute-start.5
  791.6 4.7 copy-start.3
where the time goes:
time: 816 us; the launch traced here: 805 us
  matrix products  300 us (37%)
  waiting for transfers between devices  218 us (27%)
  local copies, waits for them, and re-layouts  124 us (15%)
  other arithmetic  98 us (12%)
  blocking collectives  32.6 us (4%)
  starting transfers between devices  31.2 us (4%)
    dot_general x6, matrix products, contract(): jnp.einsum(pattern, left, right, precision=lax.Precision.HIGHEST, preferr...  300 us
    all_to_all x1, waiting for transfers between devices, demag_field(): lax.all_to_all(across, 'space', split_axis=2, concat_axis=4, tiled=True)  112 us
    all_to_all x3, local copies, waits for them, and re-layouts, demag_field(): lax.all_to_all(response, 'space', split_axis=4, concat_axis=2, tiled=True)  47.5 us
    all_to_all x1, waiting for transfers between devices, demag_field(): lax.all_to_all(response, 'space', split_axis=4, concat_axis=2, tiled=True)  47 us
    add x1, other arithmetic, demag_field(): kernel[0][:, None] * spec_x + kernel[3][:, None] * spec_y  42.9 us
    ppermute x3, waiting for transfers between devices, extended(): lax.ppermute(tail, axis, [(i, (i + 1) % count) for i in range(ends)])  36.4 us
    transpose x2, local copies, waits for them, and re-layouts, contract(): jnp.einsum(pattern, left, right, precision=lax.Precision.HIGHEST, preferr...  31.7 us
    ppermute x3, waiting for transfers between devices, extended(): lax.ppermute(head, axis, [((i + 1) % count, i) for i in range(ends)])  22.5 us
  transfers between devices with their start and end apart: 8, of which 5 were waited for; matrix products, arithmetic and copies ran while one was open for 6% of the time, Pallas kernels for 0%

commit v1 on v0

--- a/solution.py
+++ b/solution.py
@@ -1,8 +1,12 @@
+import functools
 import math
 
 import jax
 import jax.numpy as jnp
+import numpy as np
 from jax import lax
+from jax.experimental import pallas as pl
+from jax.experimental.pallas import tpu as pltpu
 from jax.sharding import PartitionSpec as P
 
 exchange_strength = 0.25
@@ -66,81 +70,283 @@
     return (weight_next, weight_prior)
 
 
-def phase_pair(count_in, count_out, length, flipped):
-    row_index = lax.broadcasted_iota(jnp.int32, (count_in, count_out), 0)
-    column_index = lax.broadcasted_iota(jnp.int32, (count_in, count_out), 1)
-    phase_angle = (row_index * column_index % length).astype(jnp.float32) * (2.0 * math.pi / length)
-    return (jnp.cos(phase_angle), flipped * jnp.sin(phase_angle))
-
-
-def real_table(count_in, count_out, length):
-    cosine, sine_value = phase_pair(count_in, count_out, length, -1.0)
-    return jnp.stack([cosine, sine_value])
-
-
-def complex_table(count_in, count_out, length, flipped):
-    cosine, sine_value = phase_pair(count_in, count_out, length, flipped)
-    upper_block = jnp.stack([cosine, sine_value])
-    lower_block = jnp.stack([-sine_value, cosine])
-    return jnp.stack([upper_block, lower_block])
-
-
-def real_part_table(count_in, count_out, length):
-    cosine, sine_value = phase_pair(count_in, count_out, length, 1.0)
-    return jnp.stack([cosine, -sine_value])
-
-
-def contract(pattern, left, right):
-    return jnp.einsum(
-        pattern, left, right, precision=lax.Precision.HIGHEST, preferred_element_type=jnp.float32
-    )
+def split_limbs(values):
+    upper = values.astype(jnp.bfloat16)
+    return upper, (values - upper.astype(jnp.float32)).astype(jnp.bfloat16)
+
+
+def table_limbs(table):
+    upper = table.astype(np.float32).astype(jnp.bfloat16)
+    lower = (table - upper.astype(np.float64)).astype(np.float32).astype(jnp.bfloat16)
+    return np.stack([upper, lower])
+
+
+def parity_table(count):
+    position = np.arange(count)[:, None]
+    slot = np.arange(count)[None, :]
+    turn = np.pi / count
+    even_part = np.cos(turn * (position * slot % (2 * count)))
+    odd_part = np.sin(turn * (position * slot % (2 * count)))
+    odd_part[:, 0] = np.cos(turn * (position[:, 0] * count % (2 * count)))
+    return np.concatenate([even_part, odd_part], axis=1)
+
+
+def parity_weights(count):
+    weights = np.full((2 * count,), 2.0)
+    weights[0] = 1.0
+    weights[count] = 1.0
+    return weights
+
+
+def times(value, factor):
+    re, im = value
+    wr, wi = factor
+    if wi == 0.0:
+        return (re, im) if wr == 1.0 else (wr * re, wr * im)
+    if wr == 0.0:
+        return (-im, re) if wi == 1.0 else (-wi * im, wi * re)
+    return (wr * re - wi * im, wr * im + wi * re)
+
+
+def unit_root(index, length, sign):
+    quarter = {0: (1.0, 0.0), 1: (0.0, 1.0), 2: (-1.0, 0.0), 3: (0.0, -1.0)}
+    if 4 * index % length == 0:
+        wr, wi = quarter[4 * index // length % 4]
+        return (wr, sign * wi)
+    phase = 2.0 * math.pi * index / length
+    return (math.cos(phase), sign * math.sin(phase))
+
+
+def add_pair(first, second):
+    return (first[0] + second[0], first[1] + second[1])
+
+
+def sub_pair(first, second):
+    return (first[0] - second[0], first[1] - second[1])
+
+
+def fourier(values, sign):
+    length = len(values)
+    if length == 1:
+        return values
+    evens = fourier(values[0::2], sign)
+    odds = fourier(values[1::2], sign)
+    half = length // 2
+    turned = [times(odds[k], unit_root(k, length, sign)) for k in range(half)]
+    return [add_pair(evens[k], turned[k]) for k in range(half)] + [
+        sub_pair(evens[k], turned[k]) for k in range(half)
+    ]
+
+
+def layers_to_planes(in_ref, out_ref):
+    layer_count = in_ref.shape[2]
+    row_step = 8
+
+    def chunk(i, carry):
+        rows = pl.ds(pl.multiple_of(i * row_step, row_step), row_step)
+        layers = [(in_ref[0, 0, z, rows, :], in_ref[1, 0, z, rows, :]) for z in range(layer_count)]
+        turned = [times(layers[z], unit_root(z, 2 * layer_count, -1.0)) for z in range(layer_count)]
+        evens = fourier(layers, -1.0)
+        odds = fourier(turned, -1.0)
+        for k in range(layer_count):
+            for part in range(2):
+                out_ref[2 * k, 0, part, rows, :] = evens[k][part]
+                out_ref[2 * k + 1, 0, part, rows, :] = odds[k][part]
+        return carry
+
+    lax.fori_loop(0, in_ref.shape[3] // row_step, chunk, 0)
+
+
+def planes_to_layers(scale, in_ref, out_ref):
+    layer_count = out_ref.shape[2]
+    row_step = 8
+
+    def chunk(i, carry):
+        rows = pl.ds(pl.multiple_of(i * row_step, row_step), row_step)
+        planes = [
+            (in_ref[k, 0, 0, rows, :], in_ref[k, 0, 1, rows, :]) for k in range(2 * layer_count)
+        ]
+        evens = fourier(planes[0::2], 1.0)
+        odds = fourier(planes[1::2], 1.0)
+        for z in range(layer_count):
+            total = add_pair(evens[z], times(odds[z], unit_root(z, 2 * layer_count, 1.0)))
+            out_ref[0, 0, z, rows, :] = scale * total[0]
+            out_ref[1, 0, z, rows, :] = scale * total[1]
+        return carry
+
+    lax.fori_loop(0, out_ref.shape[3] // row_step, chunk, 0)
+
+
+def dot32(left, right):
+    return jnp.dot(left, right, preferred_element_type=jnp.float32)
+
+
+def plane_kernel(
+    in_ref, kernel_ref, fy_ref, fx_ref, gx_ref, gy_ref, out_ref, spec_ref
+):
+    groups, slab = in_ref.shape[0], in_ref.shape[4]
+    rows_full = groups * slab
+    columns_full = in_ref.shape[5]
+
+    fy = jnp.concatenate([fy_ref[0], fy_ref[0], fy_ref[1]], axis=0)
+    fx = jnp.concatenate([fx_ref[0], fx_ref[0], fx_ref[1]], axis=1)
+    gx = jnp.concatenate([gx_ref[0], gx_ref[0], gx_ref[1]], axis=1)
+    gy = jnp.concatenate([gy_ref[0], gy_ref[0], gy_ref[1]], axis=0)
+
+    def forward(f, carry):
+        c, part = f // 2, f % 2
+        cells = jnp.concatenate([in_ref[g, 0, c, part] for g in range(groups)], axis=0)
+        upper, lower = split_limbs(cells)
+        lines = dot32(jnp.concatenate([upper, lower, upper], axis=1), fy)
+        upper, lower = split_limbs(lines)
+        spec_ref[f] = dot32(fx, jnp.concatenate([upper, lower, upper], axis=0))
+        return carry
+
+    lax.fori_loop(0, 6, forward, 0)
+
+    lane = 128
+    sub = 8
+    row_pos = lax.broadcasted_iota(jnp.int32, (sub, lane), 0)
+    lane_pos = lax.broadcasted_iota(jnp.int32, (sub, lane), 1)
+
+    def tensor(i, carry):
+        row_start = pl.multiple_of(i * sub, sub)
+        top = (row_pos + row_start) == 0
+        for start in range(0, columns_full, lane):
+
+            def pick(component, odd_x, odd_y):
+                def at(rows):
+                    inner = kernel_ref[component, 0, rows, start : start + lane]
+                    if odd_y and start == 0:
+                        edge = kernel_ref[component, 0, rows, columns_full : columns_full + lane]
+                        inner = jnp.where(lane_pos == 0, edge, inner)
+                    return inner
+
+                values = at(pl.ds(row_start, sub))
+                if odd_x:
+                    values = jnp.where(top, at(pl.ds(rows_full, sub)), values)
+                return values
+
+            spec = {}
+            for px in range(2):
+                for py in range(2):
+                    for f in range(6):
+                        spec[px, py, f] = spec_ref[
+                            f,
+                            pl.ds(row_start + px * rows_full, sub),
+                            py * columns_full + start : py * columns_full + start + lane,
+                        ]
+            k_xy = pick(3, 0, 0)
+            for px in range(2):
+                for py in range(2):
+                    sx = 1.0 if px else -1.0
+                    sy = 1.0 if py else -1.0
+                    k_xx, k_yy, k_zz = [pick(n, px, py) for n in range(3)]
+                    k_xz = sx * pick(4, 0, py)
+                    k_yz = sy * pick(5, px, 0)
+                    xy_both = -(sx * sy) * k_xy
+                    for part in range(2):
+                        turn = 1.0 if part else -1.0
+                        other = 1 - part
+                        field_x = (
+                            k_xx * spec[px, py, part]
+                            + xy_both * spec[1 - px, 1 - py, 2 + part]
+                            + turn * (k_xz * spec[1 - px, py, 4 + other])
+                        )
+                        field_y = (
+                            xy_both * spec[1 - px, 1 - py, part]
+                            + k_yy * spec[px, py, 2 + part]
+                            + turn * (k_yz * spec[px, 1 - py, 4 + other])
+                        )
+                        field_z = k_zz * spec[px, py, 4 + part] + turn * (
+                            k_xz * spec[1 - px, py, other] + k_yz * spec[px, 1 - py, 2 + other]
+                        )
+                        for c, field in enumerate((field_x, field_y, field_z)):
+                            spec_ref[
+                                2 * c + part,
+                                pl.ds(row_start + px * rows_full, sub),
+                                py * columns_full + start : py * columns_full + start + lane,
+                            ] = field
+        return carry
+
+    lax.fori_loop(0, rows_full // sub, tensor, 0)
+
+    def backward(f, carry):
+        c, part = f // 2, f % 2
+        upper, lower = split_limbs(spec_ref[f])
+        lines = dot32(gx, jnp.concatenate([upper, lower, upper], axis=0))
+        upper, lower = split_limbs(lines)
+        cells = dot32(jnp.concatenate([upper, lower, upper], axis=1), gy)
+        for g in range(groups):
+            out_ref[g, 0, c, part] = cells[g * slab : (g + 1) * slab]
+        return carry
+
+    lax.fori_loop(0, 6, backward, 0)
+
+
+def demag_pair(magnet, kernel):
+    layer_count, row_count, column_count = magnet.shape[2:]
+    groups = lax.axis_size("space")
+    local_planes = 2 * layer_count // groups
+    full_rows = row_count * groups
+    plane_dims = (2 * layer_count, 3, 2, row_count, column_count)
+    layer_spec = pl.BlockSpec((2, 1, layer_count, row_count, column_count), lambda c: (0, c, 0, 0, 0))
+    plane_spec = pl.BlockSpec((2 * layer_count, 1, 2, row_count, column_count), lambda c: (0, c, 0, 0, 0))
+    planes = pl.pallas_call(
+        layers_to_planes,
+        grid=(3,),
+        in_specs=[layer_spec],
+        out_specs=plane_spec,
+        out_shape=jax.ShapeDtypeStruct(plane_dims, jnp.float32),
+        name="layers_to_planes",
+    )(magnet)
+    planes = lax.all_to_all(planes, "space", split_axis=0, concat_axis=0, tiled=True)
+    planes = planes.reshape((groups, local_planes) + plane_dims[1:])
+    table_y = parity_table(column_count)
+    table_x = parity_table(full_rows)
+    tables = [
+        table_limbs(table_y),
+        table_limbs(table_x.T),
+        table_limbs(table_x * parity_weights(full_rows)[None, :]),
+        table_limbs((table_y * parity_weights(column_count)[None, :]).T),
+    ]
+    slab_spec = pl.BlockSpec(
+        (groups, 1, 3, 2, row_count, column_count), lambda q: (0, q, 0, 0, 0, 0)
+    )
+    kernel_spec = pl.BlockSpec(
+        (6, 1, full_rows + 8, column_count + 128), lambda q: (0, q, 0, 0)
+    )
+    whole_spec = [pl.BlockSpec(t.shape, lambda q: (0, 0, 0)) for t in tables]
+    planes = pl.pallas_call(
+        plane_kernel,
+        grid=(local_planes,),
+        in_specs=[slab_spec, kernel_spec] + whole_spec,
+        out_specs=slab_spec,
+        out_shape=jax.ShapeDtypeStruct(planes.shape, jnp.float32),
+        scratch_shapes=[
+            pltpu.VMEM((6, 2 * full_rows, 2 * column_count), jnp.float32),
+        ],
+        compiler_params=pltpu.CompilerParams(vmem_limit_bytes=60 * 1024 * 1024),
+        name="plane_kernel",
+    )(planes, kernel, *[jnp.asarray(t) for t in tables])
+    planes = planes.reshape(plane_dims)
+    planes = lax.all_to_all(planes, "space", split_axis=0, concat_axis=0, tiled=True)
+    padded_cells = 8 * layer_count * full_rows * column_count
+    return pl.pallas_call(
+        functools.partial(planes_to_layers, -1.0 / padded_cells),
+        grid=(3,),
+        in_specs=[plane_spec],
+        out_specs=layer_spec,
+        out_shape=jax.ShapeDtypeStruct(magnet.shape, jnp.float32),
+        name="planes_to_layers",
+    )(planes)
 
 
 def demag_field(magnet, kernel):
-    layer_count = magnet.shape[2]
-    column_count = magnet.shape[4]
-    full_rows = kernel.shape[2] // 2
-    across = contract(
-        "bczxy,szq->bcqsxy", magnet, real_table(layer_count, 2 * layer_count, 2 * layer_count)
-    )
-    planes = lax.all_to_all(across, "space", split_axis=2, concat_axis=4, tiled=True)
-    planes = contract(
-        "bcqrxy,rsyv->bcqsxv",
-        planes,
-        complex_table(column_count, 2 * column_count, 2 * column_count, -1.0),
-    )
-    spectrum = contract(
-        "bcqrxv,rsxu->bcqsuv", planes, complex_table(full_rows, 2 * full_rows, 2 * full_rows, -1.0)
-    )
-    spec_x = spectrum[:, 0]
-    spec_y = spectrum[:, 1]
-    spec_z = spectrum[:, 2]
-    field_x = (
-        kernel[0][:, None] * spec_x + kernel[3][:, None] * spec_y + kernel[4][:, None] * spec_z
-    )
-    field_y = (
-        kernel[3][:, None] * spec_x + kernel[1][:, None] * spec_y + kernel[5][:, None] * spec_z
-    )
-    field_z = (
-        kernel[4][:, None] * spec_x + kernel[5][:, None] * spec_y + kernel[2][:, None] * spec_z
-    )
-    response = jnp.stack([field_x, field_y, field_z], axis=1)
-    response = contract(
-        "bcqrxv,rsxu->bcqsuv", response, complex_table(2 * full_rows, full_rows, 2 * full_rows, 1.0)
-    )
-    response = contract(
-        "bcqrxv,rsvy->bcqsxy",
-        response,
-        complex_table(2 * column_count, column_count, 2 * column_count, 1.0),
-    )
-    returned = lax.all_to_all(response, "space", split_axis=4, concat_axis=2, tiled=True)
-    result = contract(
-        "bcqsxy,sqz->bczxy",
-        returned,
-        real_part_table(2 * layer_count, layer_count, 2 * layer_count),
-    )
-    padded_cells = 8 * layer_count * full_rows * column_count
-    return result * (-1.0 / padded_cells)
+    pairs = [
+        demag_pair(magnet[start : start + 2], kernel) for start in range(0, magnet.shape[0], 2)
+    ]
+    return pairs[0] if len(pairs) == 1 else jnp.concatenate(pairs, axis=0)
 
 
 def local_fields(magnet, anisotropy, kernel):

time: 816 us -> 309 us (0.38); the launches traced: 805 us -> 309 us
  matrix products: 300 us -> 0 us
  waiting for transfers between devices: 218 us -> 46.5 us
  local copies, waits for them, and re-layouts: 124 us -> 10.1 us
  Pallas kernels: 0 us -> 73.1 us
  blocking collectives: 32.6 us -> 103 us
  other arithmetic: 98 us -> 52.2 us
    dot_general x6 -> x0, matrix products: 300 us -> none  [contract(): jnp.einsum(pattern, left, right, precision=lax.Precision.HIGHEST, preferr...]
    all_to_all x2 -> x1, waiting for transfers between devices: 159 us -> 46.5 us  [demag_pair(): lax.all_to_all(planes, 'space', split_axis=0, concat_axis=0, tiled=True)]
    all_to_all x0 -> x1, blocking collectives: none -> 78 us  [demag_pair(): lax.all_to_all(planes, 'space', split_axis=0, concat_axis=0, tiled=True)]
    pallas_call x0 -> x3, Pallas kernels: none -> 73.1 us  [the longest x1 61.6 us: demag_pair(): pl.pallas_call(plane_kernel, grid=(local_planes,), in_specs=[slab_spec, k...]
    all_to_all x4 -> x0, local copies, waits for them, and re-layouts: 58.8 us -> none  [the longest x3 47.5 us: demag_field(): lax.all_to_all(response, 'space', split_axis=4, concat_axis=2, tiled=True)]
    add x1 -> x0, other arithmetic: 42.9 us -> none  [demag_field(): kernel[0][:, None] * spec_x + kernel[3][:, None] * spec_y]
    ppermute x3, waiting for transfers between devices: 36.4 us -> 0.01 us  [extended(): lax.ppermute(tail, axis, [(i, (i + 1) % count) for i in range(ends)])]
    transpose x2 -> x0, local copies, waits for them, and re-layouts: 31.7 us -> none  [contract(): jnp.einsum(pattern, left, right, precision=lax.Precision.HIGHEST, preferr...]
  transfers between devices with their start and end apart: 8 -> 7, of which waited for: 5 -> 1; matrix products, arithmetic and copies ran while one was open for 6% -> 7% of each run, Pallas kernels for 0% -> 2%
where the time goes in v1:
time: 309 us
  blocking collectives  103 us (33%)
  Pallas kernels  73.1 us (24%)
  other arithmetic  52.2 us (17%)
  waiting for transfers between devices  46.5 us (15%)
  starting transfers between devices  23.1 us (7%)
  local copies, waits for them, and re-layouts  10.1 us (3%)
    all_to_all x1, blocking collectives, demag_pair(): lax.all_to_all(planes, 'space', split_axis=0, concat_axis=0, tiled=True)  78 us
    pallas_call x1, Pallas kernels, demag_pair(): pl.pallas_call(plane_kernel, grid=(local_planes,), in_specs=[slab_spec, k...  61.6 us
    all_to_all x1, waiting for transfers between devices, demag_pair(): lax.all_to_all(planes, 'space', split_axis=0, concat_axis=0, tiled=True)  46.5 us
    ppermute x3, starting transfers between devices, extended(): lax.ppermute(tail, axis, [(i, (i + 1) % count) for i in range(ends)])  13.7 us
    psum x1, blocking collectives, body(): lax.psum((energy_part, next_part, prior_part), 'space')  12.2 us
    reduce_sum x1, other arithmetic, angle_squared(): cosine = jnp.sum(first * second, axis=1)  12 us
    reduce_sum x3, other arithmetic, total_cells(): return jnp.sum(values, axis=tuple(range(1, values.ndim)))  9.06 us
    sub x2, other arithmetic, angle_squared(): normal_part = jnp.cross(first, second, axis=1)  8.85 us
  transfers between devices with their start and end apart: 7, of which 1 were waited for; matrix products, arithmetic and copies ran while one was open for 7% of the time, Pallas kernels for 2%

profile of v1, /device:TPU:0, one launch (start us, length us, event | category | flops | bytes accessed | tf_op | source)
XLA Modules:
  0.0 308.5 jit_solution(11241763977532308226)
XLA Ops:
  0.6 5.6 %layers_to_planes.1 = f32[16,3,2,64,256]{4,3,2,1,0:T(8,128)} custom-call(f32[2,3,8,64,256]{4,3,2,1,0:T(8,128)} %in_ref.1), custom_call_target="tpu_custom_call" | custom-call | tf_op jit(solution)/shard_map/layers_to_planes/pallas_call | solution.py:295
  6.2 78.0 %all_to_all.10 = f32[16,3,2,64,256]{4,3,2,1,0:T(8,128)} all-to-all(f32[16,3,2,64,256]{4,3,2,1,0:T(8,128)} %layers_to_planes.1), channel_id=1, replica_groups=mesh['image'=8,'space'=4] {'space'}, dimensions={0} | all-to-all | bytes 12582912 | tf_op jit(solution)/shard_map/all_to_all | solution.py:303
  84.2 61.6 %plane_kernel.1 = f32[4,4,3,2,64,256]{5,4,3,2,1,0:T(8,128)} custom-call(f32[4,4,3,2,64,256]{5,4,3,2,1,0:T(8,128)} %bitcast.85, f32[6,4,512,512]{3,2,1,0:T(8,128)} %kernel_ref.1, bf16[2,256,512]{2,1,0:T(8,128)(2,1)} %constant.65.clone.fy_ref, bf16[2,512,256]{2,1,0:T(8,128)(2,1)} %constant.66.clone.fx_ref, bf16[2,256,512]{2,1,0:T(8,128)(2,1)} %constant.67.clone.gx_ref, ...), custom_call_target="tpu_custom_call" | custom-call | tf_op jit(solution)/shard_map/plane_kernel/pallas_call | solution.py:320
  145.8 5.5 %all-to-all-start.1 = ((f32[16,3,2,64,256]{4,3,2,1,0:T(8,128)}), f32[16,3,2,64,256]{4,3,2,1,0:T(8,128)}, u32[]{:S(2)}, u32[]{:S(2)}) async-start(f32[16,3,2,64,256]{4,3,2,1,0:T(8,128)} %bitcast.84), calls=%async_computation.1 | async-start | bytes 12582912 | tf_op jit(solution)/shard_map/all_to_all | solution.py:333
  151.3 0.0 copy-done
  151.3 2.0 fusion.52
  153.4 1.3 collective-permute-start.2
  154.6 5.9 %collective-permute-start.3 = (f32[1,3,8,64,256]{4,3,2,1,0:T(8,128)}, f32[1,3,8,64,256]{4,3,2,1,0:T(8,128)}, u32[]{:S(2)}, u32[]{:S(2)}) collective-permute-start(f32[1,3,8,64,256]{4,3,2,1,0:T(8,128)} %get-tuple-element.39), channel_id=1, source_target_pairs={{0,4},{4,8},{8,12},{12,16},{16,20},{20,24},{24,28},{1,5},{5,9},{9,... | collective-permute-start | bytes 4718600 | tf_op jit(solution)/shard_map/ppermute | solution.py:28
  160.6 0.1 fusion.51
  160.7 2.1 collective-permute-start.1
  162.7 1.3 collective-permute-start
  164.1 0.0 copy-start.14
  164.1 2.1 constant_dynamic-update-slice_fusion
  166.2 0.0 copy-done.14
  166.2 1.0 add_subtract_fusion
  167.2 2.0 copy.39
  169.2 0.0 collective-permute-done
  169.2 1.9 dynamic-update-slice.1
  171.1 0.0 collective-permute-done.1
  171.1 4.4 %fusion.33 = (f32[2,1,8,64,256]{4,3,2,1,0:T(8,128)}, f32[2,1,8,64,256]{4,3,2,1,0:T(8,128)}, f32[2,1,8,64,256]{4,3,2,1,0:T(8,128)}) fusion(f32[2,3,8,64,256]{4,3,2,1,0:T(8,128)S(1)} %copy-done, f32[2,3,8,1,256]{4,3,2,1,0:T(1,128)S(1)} %collective-permute-done.1, f32[2,3,8,65,256]{4,3,2,1,0:T(8,128)} %dynamic-update-slice.1, f32[64]{0:T(128)S(1)} %broadcast_multiply_fusion.2), kind=kLoop, calls=%fused_computation.60 | loop fusion | flops 3145728 | bytes 9486848 | tf_op jit(solution)/shard_map/mul | solution.py:385
  175.5 46.5 %all-to-all-done.1.in_ref = f32[16,3,2,64,256]{4,3,2,1,0:T(8,128)} async-done(((f32[16,3,2,64,256]{4,3,2,1,0:T(8,128)}), f32[16,3,2,64,256]{4,3,2,1,0:T(8,128)}, u32[]{:S(2)}, u32[]{:S(2)}) %all-to-all-start.1) | async-done | bytes 6291488 | tf_op jit(solution)/shard_map/all_to_all | solution.py:333
  222.0 6.0 %planes_to_layers.1 = f32[2,3,8,64,256]{4,3,2,1,0:T(8,128)} custom-call(f32[16,3,2,64,256]{4,3,2,1,0:T(8,128)} %all-to-all-done.1.in_ref), custom_call_target="tpu_custom_call" | custom-call | tf_op jit(solution)/shard_map/planes_to_layers/pallas_call | solution.py:335
  228.0 0.0 collective-permute-done.2
  228.0 0.0 collective-permute-done.3
  228.0 12.0 %fusion.26 = (f32[2,8,64,256]{3,2,1,0:T(8,128)}, f32[2,8,64,256]{3,2,1,0:T(8,128)}, f32[2,8,64,256]{3,2,1,0:T(8,128)}, f32[2,8,64,256]{3,2,1,0:T(8,128)}, f32[2]...) fusion(f32[2,3,8,64,256]{4,3,2,1,0:T(8,128)S(1)} %copy-done, ...), kind=kLoop, calls=%fused_computation.40 | loop fusion | flops 20709374 | bytes 30982152 | tf_op jit(solution)/shard_map/reduce_sum | solution.py:52
  240.0 6.9 %subtract_bitcast_fusion.1 = (f32[1,2,8,64,256]{4,3,2,1,0:T(8,128)}, f32[1,2,8,64,256]{4,3,2,1,0:T(8,128)}, f32[1,2,8,64,256]{4,3,2,1,0:T(8,128)}, f32[1,2,8,64,256]{4,3,2,1,0:T(8,128)}) fusion(f32[2,8,64,256,3]{3,2,1,4,0:T(8,128)} %get-tuple-element.30, f32[2,8,64,256,3]{3,2,1,0,4:T(8,128)} %bitcast.86, f32[2,8,64,256,3]{3,2,1,4,0:T(8,128)} %get-tuple-element.31), kind=kLoop, calls=%fused_computation.86 | loop fusion | flops 3145728 | bytes 13631488 | tf_op jit(solution)/shard_map/jit(cross)/sub | solution.py:50
  246.9 0.0 copy-done.3
  246.9 0.0 copy-done.4
  246.9 1.1 copy-done.5
  248.0 1.9 fusion.45
  249.9 12.2 %psum.37 = f32[2]{0:T(128)S(1)} all-reduce(f32[2]{0:T(128)S(1)} %broadcast_multiply_fusion), channel_id=1, replica_groups=mesh['image'=8,'space'=4] {'space'}, use_global_device_ids=true, to_apply=%region_10.12 | all-reduce | flops 2 | bytes 16 | tf_op jit(solution)/shard_map/psum | solution.py:406
  262.1 0.7 fusion.53
  262.8 1.3 collective-permute-start.4
  264.1 5.7 %collective-permute-start.5 = (f32[1]{0:T(128)}, f32[1]{0:T(128)}, u32[]{:S(2)}, u32[]{:S(2)}) collective-permute-start(f32[1]{0:T(128)} %get-tuple-element.49), channel_id=1, source_target_pairs={{0,4},{4,8},{8,12},{12,16},{16,20},{20,24},{24,28},{1,5},{5,9},{9,... | collective-permute-start | bytes 20 | tf_op jit(solution)/shard_map/ppermute | solution.py:28
  269.8 2.5 fusion.30
  272.3 0.0 copy-done.10
  272.3 0.0 copy-start.9
  272.3 1.9 multiply_reduce_fusion.6
  274.3 0.0 copy-done.11
  274.3 0.0 copy-done.12
  274.3 0.0 copy-done.13
  274.3 0.0 copy-start.1
  274.3 0.0 copy-start.6
  274.3 0.0 copy-start.7
  274.3 0.0 copy-start.8
  274.3 0.4 fusion.28
  274.7 0.0 copy-done.9
  274.7 1.9 multiply_reduce_fusion.7
  276.6 0.0 collective-permute-done.4
  276.7 0.0 collective-permute-done.5
  276.7 1.3 pad_maximum_fusion.3
  277.9 0.5 select_select_fusion.1
  278.4 0.0 copy-done.1
  278.4 0.0 copy-done.6
  278.4 0.0 copy-done.7
  278.5 5.2 %multiply_reduce_fusion.3 = (f32[2]{0:T(128)S(1)}, f32[2]{0:T(128)S(1)}, f32[2,3,8,64,256]{4,3,2,1,0:T(8,128)}) fusion(f32[2,3,8,64,256]{4,3,2,1,0:T(8,128)S(1)} %copy-done.1, f32[2,3,8,64,256]{4,3,2,1,0:T(8,128)S(1)} %copy-done, f32[2,8,64,256]{3,2,1,0:T(8,128)S(1)} %copy-done.6, f32[2,8,64,256]{3,2,1,0:T(8,128)S(1)} %copy-done.8, ...), kind=kLoop, calls=%fused_computation.53 | loop fusion | flops 13369340 | bytes 15728672 | tf_op jit(solution)/shard_map/reduce_sum | solution.py:42
  283.6 5.6 %all-reduce.1 = (f32[2]{0:T(128)S(1)}, f32[2]{0:T(128)S(1)}, f32[2]{0:T(128)S(1)}, f32[2]{0:T(128)S(1)}) all-reduce(f32[2]{0:T(128)S(1)} %get-tuple-element.15, f32[2]{0:T(128)S(1)} %get-tuple-element.14, f32[2]{0:T(128)S(1)} %multiply_reduce_fusion.6, f32[2]{0:T(128)S(1)} %multiply_reduce_fusion.7), channel_id=1, replica_groups=mesh['image'=8,'space'=4] {'space'}, use_global_device_ids=true, to_apply=%region_16.18 | all-reduce | flops 8 | bytes 64 | tf_op jit(solution)/shard_map/psum | solution.py:412
  289.3 6.4 %multiply_reduce_fusion.1 = (f32[2,8,64,256]{3,2,1,0:T(8,128)S(1)}, f32[2,3,8,64,256]{4,3,2,1,0:T(8,128)}) fusion(f32[2,3,8,64,256]{4,3,2,1,0:T(8,128)} %get-tuple-element.22, f32[2]{0:T(128)S(1)} %get-tuple-element.45, f32[2]{0:T(128)S(1)} %get-tuple-element.44, f32[2,3,8,64,256]{4,3,2,1,0:T(8,128)} %get-tuple-element.23, ...), kind=kLoop, calls=%fused_computation.50 | loop fusion | flops 6029312 | bytes 14680082 | tf_op jit(solution)/shard_map/reduce_sum | solution.py:427
  295.7 0.4 sqrt_reduce_fusion
  296.1 6.7 %pmax.7 = f32[2]{0:T(128)S(1)} all-reduce(f32[2]{0:T(128)S(1)} %sqrt_reduce_fusion), channel_id=1, replica_groups=mesh['image'=8,'space'=4] {'space'}, use_global_device_ids=true, to_apply=%region_19.21 | all-reduce | flops 2 | bytes 16 | tf_op jit(solution)/shard_map/pmax | solution.py:428
  302.8 3.0 multiply_reduce_fusion
  305.8 0.2 sqrt.32
  306.0 0.0 copy-done.2
  306.0 2.5 broadcast_divide_fusion
  (18 shorter events, 0.1 us)
Async XLA Ops:
  145.8 5.5 %copy-start = (f32[2,3,8,64,256]{4,3,2,1,0:T(8,128)S(1)}, f32[2,3,8,64,256]{4,3,2,1,0:T(8,128)}, u32[]{:S(2)}) copy-start(f32[2,3,8,64,256]{4,3,2,1,0:T(8,128)} %in_ref.1) | copy-start | bytes 9437188
  145.8 76.2 %all-to-all-start.1 = ((f32[16,3,2,64,256]{4,3,2,1,0:T(8,128)}), f32[16,3,2,64,256]{4,3,2,1,0:T(8,128)}, u32[]{:S(2)}, u32[]{:S(2)}) async-start(f32[16,3,2,64,256]{4,3,2,1,0:T(8,128)} %bitcast.84), calls=%async_computation.1 | async-start | bytes 12582912 | tf_op jit(solution)/shard_map/all_to_all | solution.py:333
  153.4 74.6 %collective-permute-start.2 = (f32[1,3,8,64,256]{4,3,2,1,0:T(8,128)}, f32[1,3,8,64,256]{4,3,2,1,0:T(8,128)}, u32[]{:S(2)}, u32[]{:S(2)}) collective-permute-start(f32[1,3,8,64,256]{4,3,2,1,0:T(8,128)} %get-tuple-element.40), channel_id=1, source_target_pairs={{4,0},{8,4},{12,8},{16,12},{20,16},{24,20},{28,24},{5,1},{9,5},{13... | collective-permute-start | bytes 4718600 | tf_op jit(solution)/shard_map/ppermute | solution.py:30
  154.6 73.3 %collective-permute-start.3 = (f32[1,3,8,64,256]{4,3,2,1,0:T(8,128)}, f32[1,3,8,64,256]{4,3,2,1,0:T(8,128)}, u32[]{:S(2)}, u32[]{:S(2)}) collective-permute-start(f32[1,3,8,64,256]{4,3,2,1,0:T(8,128)} %get-tuple-element.39), channel_id=1, source_target_pairs={{0,4},{4,8},{8,12},{12,16},{16,20},{20,24},{24,28},{1,5},{5,9},{9,... | collective-permute-start | bytes 4718600 | tf_op jit(solution)/shard_map/ppermute | solution.py:28
  160.7 10.4 %collective-permute-start.1 = (f32[2,3,8,1,256]{4,3,2,1,0:T(1,128)S(1)}, f32[2,3,8,1,256]{4,3,2,1,0:T(1,128)S(1)}, u32[]{:S(2)}, u32[]{:S(2)}) collective-permute-start(f32[2,3,8,1,256]{4,3,2,1,0:T(1,128)S(1)} %get-tuple-element.38), channel_id=1, source_target_pairs={{0,1},{1,2},{2,3},{4,5},{5,6},{6,7},{8,9},{9,10},{10,11},{12,13},{... | collective-permute-start | bytes 147464 | tf_op jit(solution)/shard_map/ppermute | solution.py:28
  162.7 6.4 %collective-permute-start = (f32[2,3,8,1,256]{4,3,2,1,0:T(1,128)S(1)}, f32[2,3,8,1,256]{4,3,2,1,0:T(1,128)S(1)}, u32[]{:S(2)}, u32[]{:S(2)}) collective-permute-start(f32[2,3,8,1,256]{4,3,2,1,0:T(1,128)S(1)} %get-tuple-element.37), channel_id=1, source_target_pairs={{1,0},{2,1},{3,2},{5,4},{6,5},{7,6},{9,8},{10,9},{11,10},{13,12},{... | collective-permute-start | bytes 147464 | tf_op jit(solution)/shard_map/ppermute | solution.py:30
  164.1 2.1 copy-start.14
  240.0 7.0 %copy-start.3 = (f32[2,8,64,256,3]{3,2,1,4,0:T(8,128)S(1)}, f32[2,8,64,256,3]{3,2,1,4,0:T(8,128)}, u32[]{:S(2)}) copy-start(f32[2,8,64,256,3]{3,2,1,4,0:T(8,128)} %get-tuple-element.30) | copy-start | bytes 9437188
  240.0 7.0 %copy-start.4 = (f32[2,8,64,256,3]{3,2,1,4,0:T(8,128)S(1)}, f32[2,8,64,256,3]{3,2,1,4,0:T(8,128)}, u32[]{:S(2)}) copy-start(f32[2,8,64,256,3]{3,2,1,4,0:T(8,128)} %get-tuple-element.31) | copy-start | bytes 9437188
  240.0 8.0 %copy-start.5 = (f32[2,3,8,64,256]{4,3,2,0,1:T(8,128)S(1)}, f32[2,3,8,64,256]{4,3,2,0,1:T(8,128)}, u32[]{:S(2)}) copy-start(f32[2,3,8,64,256]{4,3,2,0,1:T(8,128)} %copy.39) | copy-start | bytes 9437188
  262.1 10.2 %copy-start.10 = (f32[2,8,64,256]{3,2,1,0:T(8,128)S(1)}, f32[2,8,64,256]{3,2,1,0:T(8,128)}, u32[]{:S(2)}) copy-start(f32[2,8,64,256]{3,2,1,0:T(8,128)} %get-tuple-element.11) | copy-start | bytes 3145732
  262.8 13.9 %collective-permute-start.4 = (f32[1]{0:T(128)}, f32[1]{0:T(128)}, u32[]{:S(2)}, u32[]{:S(2)}) collective-permute-start(f32[1]{0:T(128)} %get-tuple-element.48), channel_id=1, source_target_pairs={{4,0},{8,4},{12,8},{16,12},{20,16},{24,20},{28,24},{5,1},{9,5},{13... | collective-permute-start | bytes 20 | tf_op jit(solution)/shard_map/ppermute | solution.py:30
  264.1 12.6 %collective-permute-start.5 = (f32[1]{0:T(128)}, f32[1]{0:T(128)}, u32[]{:S(2)}, u32[]{:S(2)}) collective-permute-start(f32[1]{0:T(128)} %get-tuple-element.49), channel_id=1, source_target_pairs={{0,4},{4,8},{8,12},{12,16},{16,20},{20,24},{24,28},{1,5},{5,9},{9,... | collective-permute-start | bytes 20 | tf_op jit(solution)/shard_map/ppermute | solution.py:28
  269.8 4.5 %copy-start.11 = (f32[1,2,8,64,256]{4,3,2,1,0:T(8,128)S(1)}, f32[1,2,8,64,256]{4,3,2,1,0:T(8,128)}, u32[]{:S(2)}) copy-start(f32[1,2,8,64,256]{4,3,2,1,0:T(8,128)} %get-tuple-element.26) | copy-start | bytes 3145732
  269.8 4.5 %copy-start.12 = (f32[1,2,8,64,256]{4,3,2,1,0:T(8,128)S(1)}, f32[1,2,8,64,256]{4,3,2,1,0:T(8,128)}, u32[]{:S(2)}) copy-start(f32[1,2,8,64,256]{4,3,2,1,0:T(8,128)} %get-tuple-element.27) | copy-start | bytes 3145732
  269.8 4.5 %copy-start.13 = (f32[1,2,8,64,256]{4,3,2,1,0:T(8,128)S(1)}, f32[1,2,8,64,256]{4,3,2,1,0:T(8,128)}, u32[]{:S(2)}) copy-start(f32[1,2,8,64,256]{4,3,2,1,0:T(8,128)} %get-tuple-element.34) | copy-start | bytes 3145732
  272.3 2.4 copy-start.9
  274.3 4.2 %copy-start.1 = (f32[2,3,8,64,256]{4,3,2,1,0:T(8,128)S(1)}, f32[2,3,8,64,256]{4,3,2,1,0:T(8,128)}, u32[]{:S(2)}) copy-start(f32[2,3,8,64,256]{4,3,2,1,0:T(8,128)} %get-tuple-element.23) | copy-start | bytes 9437188
  274.3 4.2 %copy-start.6 = (f32[2,8,64,256]{3,2,1,0:T(8,128)S(1)}, f32[2,8,64,256]{3,2,1,0:T(8,128)}, u32[]{:S(2)}) copy-start(f32[2,8,64,256]{3,2,1,0:T(8,128)} %get-tuple-element.13) | copy-start | bytes 3145732
  274.3 4.2 %copy-start.7 = (f32[2,8,64,256]{3,2,1,0:T(8,128)S(1)}, f32[2,8,64,256]{3,2,1,0:T(8,128)}, u32[]{:S(2)}) copy-start(f32[2,8,64,256]{3,2,1,0:T(8,128)} %get-tuple-element.7) | copy-start | bytes 3145732
  274.3 4.2 %copy-start.8 = (f32[2,8,64,256]{3,2,1,0:T(8,128)S(1)}, f32[2,8,64,256]{3,2,1,0:T(8,128)}, u32[]{:S(2)}) copy-start(f32[2,8,64,256]{3,2,1,0:T(8,128)} %get-tuple-element.10) | copy-start | bytes 3145732
  302.8 3.2 %copy-start.2 = (f32[2,3,8,64,256]{4,3,2,1,0:T(8,128)S(1)}, f32[2,3,8,64,256]{4,3,2,1,0:T(8,128)}, u32[]{:S(2)}) copy-start(f32[2,3,8,64,256]{4,3,2,1,0:T(8,128)} %get-tuple-element.21) | copy-start | bytes 9437188

commit v2 on v1

--- a/solution.py
+++ b/solution.py
@@ -182,12 +182,97 @@
 
 
 def plane_kernel(
-    in_ref, kernel_ref, fy_ref, fx_ref, gx_ref, gy_ref, out_ref, spec_ref
+    planes_ref,
+    kernel_ref,
+    fy_ref,
+    fx_ref,
+    gx_ref,
+    gy_ref,
+    out_ref,
+    spec_ref,
+    held_ref,
+    tensor_ref,
+    result_ref,
+    send_sem,
+    recv_sem,
+    own_sem,
+    tensor_sem,
+    out_sem,
 ):
-    groups, slab = in_ref.shape[0], in_ref.shape[4]
+    groups, local_planes = planes_ref.shape[0], planes_ref.shape[1]
+    slab, columns_full = planes_ref.shape[4], planes_ref.shape[5]
     rows_full = groups * slab
-    columns_full = in_ref.shape[5]
-
+    me = lax.axis_index("space")
+    peers = [lax.rem(me + d, groups) for d in range(groups)]
+    sources = [lax.rem(me + groups - d, groups) for d in range(groups)]
+
+    def tensor_copy(q):
+        return pltpu.make_async_copy(
+            kernel_ref.at[:, q, pl.ds(0, rows_full + 8), pl.ds(0, columns_full + 128)],
+            tensor_ref.at[q],
+            tensor_sem.at[q],
+        )
+
+    def own_copy(q):
+        return pltpu.make_async_copy(planes_ref.at[me, q], held_ref.at[q, me], own_sem.at[q])
+
+    def out_copy(q):
+        return pltpu.make_async_copy(result_ref.at[q], out_ref.at[:, q], out_sem.at[q])
+
+    def remote_copy(q, d):
+        return pltpu.make_async_remote_copy(
+            src_ref=planes_ref.at[peers[d], q],
+            dst_ref=held_ref.at[q, me],
+            send_sem=send_sem.at[q, d],
+            recv_sem=recv_sem.at[q, d],
+            device_id={"space": peers[d]},
+            device_id_type=pl.DeviceIdType.MESH,
+        )
+
+    def arrival(q, d):
+        return pltpu.make_async_remote_copy(
+            src_ref=planes_ref.at[peers[d], q],
+            dst_ref=held_ref.at[q, sources[d]],
+            send_sem=send_sem.at[q, d],
+            recv_sem=recv_sem.at[q, d],
+            device_id={"space": peers[d]},
+            device_id_type=pl.DeviceIdType.MESH,
+        )
+
+    barrier = pltpu.get_barrier_semaphore()
+    for d in range(1, groups):
+        pl.semaphore_signal(
+            barrier, inc=1, device_id={"space": peers[d]}, device_id_type=pl.DeviceIdType.MESH
+        )
+    for q in range(local_planes):
+        tensor_copy(q).start()
+        own_copy(q).start()
+    pl.semaphore_wait(barrier, groups - 1)
+    for q in range(local_planes):
+        for d in range(1, groups):
+            remote_copy(q, d).start()
+
+    def plane(q, carry):
+        tensor_copy(q).wait()
+        own_copy(q).wait()
+        for d in range(1, groups):
+            arrival(q, d).wait_recv()
+        plane_compute(
+            held_ref.at[q], tensor_ref.at[q], fy_ref, fx_ref, gx_ref, gy_ref, result_ref.at[q], spec_ref
+        )
+        out_copy(q).start()
+        return carry
+
+    lax.fori_loop(0, local_planes, plane, 0)
+    for q in range(local_planes):
+        out_copy(q).wait()
+        for d in range(1, groups):
+            remote_copy(q, d).wait_send()
+
+
+def plane_compute(in_ref, kernel_ref, fy_ref, fx_ref, gx_ref, gy_ref, out_ref, spec_ref):
+    groups, slab, columns_full = in_ref.shape[0], in_ref.shape[3], in_ref.shape[4]
+    rows_full = groups * slab
     fy = jnp.concatenate([fy_ref[0], fy_ref[0], fy_ref[1]], axis=0)
     fx = jnp.concatenate([fx_ref[0], fx_ref[0], fx_ref[1]], axis=1)
     gx = jnp.concatenate([gx_ref[0], gx_ref[0], gx_ref[1]], axis=1)
@@ -195,7 +280,7 @@
 
     def forward(f, carry):
         c, part = f // 2, f % 2
-        cells = jnp.concatenate([in_ref[g, 0, c, part] for g in range(groups)], axis=0)
+        cells = jnp.concatenate([in_ref[g, c, part] for g in range(groups)], axis=0)
         upper, lower = split_limbs(cells)
         lines = dot32(jnp.concatenate([upper, lower, upper], axis=1), fy)
         upper, lower = split_limbs(lines)
@@ -216,9 +301,9 @@
 
             def pick(component, odd_x, odd_y):
                 def at(rows):
-                    inner = kernel_ref[component, 0, rows, start : start + lane]
+                    inner = kernel_ref[component, rows, start : start + lane]
                     if odd_y and start == 0:
-                        edge = kernel_ref[component, 0, rows, columns_full : columns_full + lane]
+                        edge = kernel_ref[component, rows, columns_full : columns_full + lane]
                         inner = jnp.where(lane_pos == 0, edge, inner)
                     return inner
 
@@ -278,13 +363,13 @@
         upper, lower = split_limbs(lines)
         cells = dot32(jnp.concatenate([upper, lower, upper], axis=1), gy)
         for g in range(groups):
-            out_ref[g, 0, c, part] = cells[g * slab : (g + 1) * slab]
+            out_ref[g, c, part] = cells[g * slab : (g + 1) * slab]
         return carry
 
     lax.fori_loop(0, 6, backward, 0)
 
 
-def demag_pair(magnet, kernel):
+def demag_pair(magnet, kernel, images, pair_index):
     layer_count, row_count, column_count = magnet.shape[2:]
     groups = lax.axis_size("space")
     local_planes = 2 * layer_count // groups
@@ -300,7 +385,6 @@
         out_shape=jax.ShapeDtypeStruct(plane_dims, jnp.float32),
         name="layers_to_planes",
     )(magnet)
-    planes = lax.all_to_all(planes, "space", split_axis=0, concat_axis=0, tiled=True)
     planes = planes.reshape((groups, local_planes) + plane_dims[1:])
     table_y = parity_table(column_count)
     table_x = parity_table(full_rows)
@@ -310,29 +394,40 @@
         table_limbs(table_x * parity_weights(full_rows)[None, :]),
         table_limbs((table_y * parity_weights(column_count)[None, :]).T),
     ]
-    slab_spec = pl.BlockSpec(
-        (groups, 1, 3, 2, row_count, column_count), lambda q: (0, q, 0, 0, 0, 0)
-    )
-    kernel_spec = pl.BlockSpec(
-        (6, 1, full_rows + 8, column_count + 128), lambda q: (0, q, 0, 0)
-    )
-    whole_spec = [pl.BlockSpec(t.shape, lambda q: (0, 0, 0)) for t in tables]
+    slab_dims = (local_planes, groups, 3, 2, row_count, column_count)
+    tensor_dims = (local_planes, 6, full_rows + 8, column_count + 128)
+    anywhere = pl.BlockSpec(memory_space=pl.ANY)
+    inside = pl.BlockSpec(memory_space=pltpu.VMEM)
+    dots = 6 * local_planes * 4 * full_rows * column_count * 3 * (full_rows + column_count // 2)
     planes = pl.pallas_call(
         plane_kernel,
-        grid=(local_planes,),
-        in_specs=[slab_spec, kernel_spec] + whole_spec,
-        out_specs=slab_spec,
+        in_specs=[anywhere, anywhere] + [inside] * len(tables),
+        out_specs=anywhere,
         out_shape=jax.ShapeDtypeStruct(planes.shape, jnp.float32),
         scratch_shapes=[
             pltpu.VMEM((6, 2 * full_rows, 2 * column_count), jnp.float32),
+            pltpu.VMEM(slab_dims, jnp.float32),
+            pltpu.VMEM(tensor_dims, jnp.float32),
+            pltpu.VMEM(slab_dims, jnp.float32),
+            pltpu.SemaphoreType.DMA((local_planes, groups)),
+            pltpu.SemaphoreType.DMA((local_planes, groups)),
+            pltpu.SemaphoreType.DMA((local_planes,)),
+            pltpu.SemaphoreType.DMA((local_planes,)),
+            pltpu.SemaphoreType.DMA((local_planes,)),
         ],
-        compiler_params=pltpu.CompilerParams(vmem_limit_bytes=60 * 1024 * 1024),
+        compiler_params=pltpu.CompilerParams(
+            vmem_limit_bytes=56 * 1024 * 1024, collective_id=pair_index, has_side_effects=True
+        ),
+        cost_estimate=pl.CostEstimate(
+            flops=4 * dots, bytes_accessed=4 * planes.size * 4, transcendentals=0
+        ),
         name="plane_kernel",
     )(planes, kernel, *[jnp.asarray(t) for t in tables])
     planes = planes.reshape(plane_dims)
+    planes, *images = lax.optimization_barrier((planes, *images))
     planes = lax.all_to_all(planes, "space", split_axis=0, concat_axis=0, tiled=True)
     padded_cells = 8 * layer_count * full_rows * column_count
-    return pl.pallas_call(
+    field = pl.pallas_call(
         functools.partial(planes_to_layers, -1.0 / padded_cells),
         grid=(3,),
         in_specs=[plane_spec],
@@ -340,16 +435,18 @@
         out_shape=jax.ShapeDtypeStruct(magnet.shape, jnp.float32),
         name="planes_to_layers",
     )(planes)
-
-
-def demag_field(magnet, kernel):
-    pairs = [
-        demag_pair(magnet[start : start + 2], kernel) for start in range(0, magnet.shape[0], 2)
-    ]
-    return pairs[0] if len(pairs) == 1 else jnp.concatenate(pairs, axis=0)
-
-
-def local_fields(magnet, anisotropy, kernel):
+    return field, images
+
+
+def demag_field(magnet, kernel, images):
+    fields = []
+    for index, start in enumerate(range(0, magnet.shape[0], 2)):
+        field, images = demag_pair(magnet[start : start + 2], kernel, images, index)
+        fields.append(field)
+    return (fields[0] if len(fields) == 1 else jnp.concatenate(fields, axis=0)), images
+
+
+def local_fields(magnet, anisotropy):
     layer_count = magnet.shape[2]
     row_count = magnet.shape[3]
     column_count = magnet.shape[4]
@@ -387,42 +484,66 @@
     chiral_z = -chiral_strength * (x_plus[:, 0] - x_minus[:, 0] + (y_plus[:, 1] - y_minus[:, 1]))
     easy_axis = 2.0 * anisotropy[:, None] * magnet[:, 2]
     local_part = exchange_part + jnp.stack([chiral_x, chiral_y, chiral_z + easy_axis], axis=1)
-    return local_part + demag_field(magnet, kernel)
+    return local_part
 
 
 def body(magnet, anisotropy, kernel):
     image_count = magnet.shape[0]
     cell_count = magnet.shape[2] * magnet.shape[3] * lax.axis_size("space") * magnet.shape[4]
-    fields = local_fields(magnet, anisotropy, kernel)
     framed = extended(magnet, (("image", 0),), 1)
+    demag, (framed,) = demag_field(magnet, kernel, [framed])
+    fields = local_fields(magnet, anisotropy) + demag
     prior_image = framed[:-2]
     next_image = framed[2:]
     true_force = project(fields, magnet)
     tangent_next = project(next_image - magnet, magnet)
     tangent_prior = project(magnet - prior_image, magnet)
-    energy_part = -0.5 * total_cells(magnet * fields)
-    next_part = total_cells(angle_squared(magnet, next_image))
-    prior_part = total_cells(angle_squared(magnet, prior_image))
-    energy_total, next_squares, prior_squares = lax.psum(
-        (energy_part, next_part, prior_part), "space"
-    )
-    framed_energy = extended(energy_total, (("image", 0),), 1)
-    weight_next, weight_prior = tangent_weights(energy_total, framed_energy[2:], framed_energy[:-2])
-    tangent = lift_axes(weight_next) * tangent_next + lift_axes(weight_prior) * tangent_prior
-    length_squares, drive_total = lax.psum(
-        (total_cells(tangent * tangent), total_cells(true_force * tangent)), "space"
-    )
-    tangent_scale = jnp.sqrt(length_squares / cell_count + epsilon)
-    unit_tangent = tangent / lift_axes(tangent_scale)
+    sums = jnp.stack(
+        [
+            -0.5 * total_cells(magnet * fields),
+            total_cells(angle_squared(magnet, next_image)),
+            total_cells(tangent_next * tangent_next),
+            total_cells(tangent_next * tangent_prior),
+            total_cells(tangent_prior * tangent_prior),
+            total_cells(true_force * tangent_next),
+            total_cells(true_force * tangent_prior),
+        ],
+        axis=1,
+    )
+    band_size = image_count * lax.axis_size("image")
+    gathered = lax.all_gather(sums, ("image", "space"))
+    gathered = gathered.reshape(
+        (lax.axis_size("image"), lax.axis_size("space")) + sums.shape
+    )
+    band = jnp.sum(gathered, axis=1).reshape(band_size, sums.shape[1])
+    energy_band, distance_band = band[:, 0], jnp.sqrt(band[:, 1] / cell_count)
+    weight_next, weight_prior = tangent_weights(
+        energy_band, jnp.roll(energy_band, -1), jnp.roll(energy_band, 1)
+    )
+    length_squares = (
+        weight_next * weight_next * band[:, 2]
+        + 2.0 * weight_next * weight_prior * band[:, 3]
+        + weight_prior * weight_prior * band[:, 4]
+    )
+    drive_total = weight_next * band[:, 5] + weight_prior * band[:, 6]
+    tangent_scale = jnp.sqrt(jnp.maximum(length_squares, 0.0) / cell_count + epsilon)
     parallel = drive_total / (cell_count * tangent_scale)
-    distance_next = jnp.sqrt(next_squares / cell_count)
-    distance_prior = jnp.sqrt(prior_squares / cell_count)
-    spring = spring_strength * (distance_next - distance_prior)
-    image_index = lax.axis_index("image") * image_count + jnp.arange(image_count)
-    band_size = image_count * lax.axis_size("image")
-    interior = (image_index > 0) & (image_index < band_size - 1)
+    spring = spring_strength * (distance_band - jnp.roll(distance_band, 1))
+    image_index = jnp.arange(band_size)
+    interior = ((image_index > 0) & (image_index < band_size - 1)).astype(jnp.float32)
+    pull = (spring - parallel) / tangent_scale
+    first_image = lax.axis_index("image") * image_count
+    mine = lax.dynamic_slice_in_dim(
+        jnp.stack([energy_band, pull * weight_next, pull * weight_prior, interior], axis=1),
+        first_image,
+        image_count,
+        axis=0,
+    )
+    energy_total = mine[:, 0]
     band_force = jnp.where(
-        lift_axes(interior), true_force + lift_axes(spring - parallel) * unit_tangent, 0.0
+        lift_axes(mine[:, 3]) > 0.0,
+        true_force + lift_axes(mine[:, 1]) * tangent_next + lift_axes(mine[:, 2]) * tangent_prior,
+        0.0,
     )
     local_largest = jnp.max(jnp.sqrt(jnp.sum(band_force * band_force, axis=1)), axis=(1, 2, 3))
     largest = lax.pmax(local_largest, "space")

time: 309 us -> 291 us (0.942)
  blocking collectives: 103 us -> 54.4 us
  Pallas kernels: 73.1 us -> 91.9 us
  waiting for transfers between devices: 46.5 us -> 51.2 us
  local copies, waits for them, and re-layouts: 10.1 us -> 14.4 us
    all_to_all x1 -> x0, blocking collectives: 78 us -> none  [demag_pair(): lax.all_to_all(planes, 'space', split_axis=0, concat_axis=0, tiled=True)]
    all_gather x0 -> x1, blocking collectives: none -> 48.4 us  [body(): gathered = lax.all_gather(sums, ('image', 'space'))]
    pallas_call x1, Pallas kernels: 61.6 us -> 80.4 us  [demag_pair(): pl.pallas_call(plane_kernel, in_specs=[anywhere, anywhere] + [inside] * l...]
    psum x2 -> x0, blocking collectives: 17.8 us -> none  [the longest x1 12.2 us: body(): lax.psum((energy_part, next_part, prior_part), 'space')]
    sub x2, other arithmetic: 8.85 us -> 3.81 us  [angle_squared(): normal_part = jnp.cross(first, second, axis=1)]
    all_to_all x1, waiting for transfers between devices: 46.5 us -> 51.2 us  [demag_pair(): lax.all_to_all(planes, 'space', split_axis=0, concat_axis=0, tiled=True)]
    all_to_all x1, starting transfers between devices: 5.49 us -> 10.1 us  [demag_pair(): lax.all_to_all(planes, 'space', split_axis=0, concat_axis=0, tiled=True)]
    concatenate x1, other arithmetic: 1.27 us -> 5.35 us  [extended(): jnp.concatenate([lax.ppermute(tail, axis, [(i, (i + 1) % count) for i in...]
  transfers between devices with their start and end apart: 7 -> 5, of which waited for: 1 -> 1; matrix products, arithmetic and copies ran while one was open for 7% -> 4% of each run, Pallas kernels for 2% -> 30%
where the time goes in v2:
time: 291 us; the launch traced here: 290 us
  Pallas kernels  91.9 us (32%)
  blocking collectives  54.4 us (19%)
  other arithmetic  53.4 us (18%)
  waiting for transfers between devices  51.2 us (18%)
  starting transfers between devices  24.2 us (8%)
  local copies, waits for them, and re-layouts  14.4 us (5%)
    pallas_call x1, Pallas kernels, demag_pair(): pl.pallas_call(plane_kernel, in_specs=[anywhere, anywhere] + [inside] * l...  80.4 us
    all_to_all x1, waiting for transfers between devices, demag_pair(): lax.all_to_all(planes, 'space', split_axis=0, concat_axis=0, tiled=True)  51.2 us
    all_gather x1, blocking collectives, body(): gathered = lax.all_gather(sums, ('image', 'space'))  48.4 us
    ppermute x2, starting transfers between devices, extended(): lax.ppermute(tail, axis, [(i, (i + 1) % count) for i in range(ends)])  11.6 us
    reduce_sum x1, other arithmetic, angle_squared(): cosine = jnp.sum(first * second, axis=1)  11.4 us
    reduce_sum x2, other arithmetic, total_cells(): return jnp.sum(values, axis=tuple(range(1, values.ndim)))  10.2 us
    all_to_all x1, starting transfers between devices, demag_pair(): lax.all_to_all(planes, 'space', split_axis=0, concat_axis=0, tiled=True)  10.1 us
    reduce_sum x1, other arithmetic, body(): jnp.sum(band_force * band_force, axis=1)  7 us
  transfers between devices with their start and end apart: 5, of which 1 were waited for; matrix products, arithmetic and copies ran while one was open for 4% of the time, Pallas kernels for 30%

profile of v2, /device:TPU:0, one launch (start us, length us, event | category | flops | bytes accessed | tf_op | source)
XLA Modules:
  0.0 290.4 jit_solution(20017507797473222)
XLA Ops:
  0.6 3.9 %fusion.46 = (f32[1,3,8,64,256]{4,3,2,1,0:T(8,128)}, f32[1,3,8,64,256]{4,3,2,1,0:T(8,128)}) fusion(f32[2,3,8,64,256]{4,3,2,1,0:T(8,128)} %in_ref.1), kind=kLoop, calls=%fused_computation.122 | loop fusion | bytes 6291456 | tf_op jit(solution)/shard_map/slice | solution.py:25
  4.5 6.0 %collective-permute-start.2 = (f32[1,3,8,64,256]{4,3,2,1,0:T(8,128)}, f32[1,3,8,64,256]{4,3,2,1,0:T(8,128)}, u32[]{:S(2)}, u32[]{:S(2)}) collective-permute-start(f32[1,3,8,64,256]{4,3,2,1,0:T(8,128)} %get-tuple-element.38), channel_id=1, source_target_pairs={{0,4},{4,8},{8,12},{12,16},{16,20},{20,24},{24,28},{1,5},{5,9},{9,... | collective-permute-start | bytes 4718600 | tf_op jit(solution)/shard_map/ppermute | solution.py:28
  10.5 1.3 collective-permute-start.3
  11.8 5.6 %layers_to_planes.1 = f32[16,3,2,64,256]{4,3,2,1,0:T(8,128)} custom-call(f32[2,3,8,64,256]{4,3,2,1,0:T(8,128)} %in_ref.1), custom_call_target="tpu_custom_call" | custom-call | tf_op jit(solution)/shard_map/layers_to_planes/pallas_call | solution.py:380
  17.4 0.0 copy-start
  17.4 80.4 %plane_kernel.1 = f32[4,4,3,2,64,256]{5,4,3,2,1,0:T(8,128)} custom-call(f32[4,4,3,2,64,256]{5,4,3,2,1,0:T(8,128)} %bitcast.63, f32[6,4,512,512]{3,2,1,0:T(8,128)} %kernel_ref.1, bf16[2,256,512]{2,1,0:T(8,128)(2,1)} %constant.70.clone.fy_ref, bf16[2,512,256]{2,1,0:T(8,128)(2,1)} %constant.71.clone.fx_ref, bf16[2,256,512]{2,1,0:T(8,128)(2,1)} %constant.72.clone.gx_ref, ...), custom_call_target="tpu_custom_call" | custom-call | flops 28991029248 | bytes 25165824 | tf_op jit(solution)/shard_map/plane_kernel/pallas_call | solution.py:402
  97.8 0.0 collective-permute-done.2
  97.8 0.0 collective-permute-done.3
  97.8 0.0 copy-done
  97.8 5.4 %pad_maximum_fusion = f32[4,3,8,64,256]{4,3,2,1,0:T(8,128)} fusion(f32[1,3,8,64,256]{4,3,2,1,0:T(8,128)} %collective-permute-done.3, f32[2,3,8,64,256]{4,3,2,1,0:T(8,128)S(1)} %copy-done, f32[1,3,8,64,256]{4,3,2,1,0:T(8,128)} %collective-permute-done.2), kind=kLoop, calls=%fused_computation.8 | loop fusion | flops 3145728 | bytes 12582912 | tf_op jit(solution)/shard_map/concatenate | solution.py:26
  103.2 10.1 %all-to-all-start = ((f32[16,3,2,64,256]{4,3,2,1,0:T(8,128)}), f32[16,3,2,64,256]{4,3,2,1,0:T(8,128)}, u32[]{:S(2)}, u32[]{:S(2)}) async-start(f32[16,3,2,64,256]{4,3,2,1,0:T(8,128)} %bitcast.62), calls=%async_computation | async-start | bytes 12582912 | tf_op jit(solution)/shard_map/all_to_all | solution.py:428
  113.2 0.1 fusion.45
  113.3 1.3 collective-permute-start
  114.6 5.5 %collective-permute-start.1 = (f32[2,3,8,1,256]{4,3,2,1,0:T(1,128)S(1)}, f32[2,3,8,1,256]{4,3,2,1,0:T(1,128)S(1)}, u32[]{:S(2)}, u32[]{:S(2)}) collective-permute-start(f32[2,3,8,1,256]{4,3,2,1,0:T(1,128)S(1)} %get-tuple-element.37), channel_id=1, source_target_pairs={{0,1},{1,2},{2,3},{4,5},{5,6},{6,7},{8,9},{9,10},{10,11},{12,13},{... | collective-permute-start | bytes 147464 | tf_op jit(solution)/shard_map/ppermute | solution.py:28
  120.2 0.0 copy-start.5
  120.2 2.0 constant_dynamic-update-slice_fusion
  122.2 0.0 copy-done.5
  122.3 0.9 add_subtract_fusion
  123.2 2.0 copy.70
  125.2 0.0 collective-permute-done
  125.2 1.9 dynamic-update-slice.1
  127.1 0.0 collective-permute-done.1
  127.1 4.5 %fusion.13 = (f32[2,1,8,64,256]{4,3,2,1,0:T(8,128)}, f32[2,1,8,64,256]{4,3,2,1,0:T(8,128)}, f32[2,1,8,64,256]{4,3,2,1,0:T(8,128)}) fusion(f32[2,3,8,64,256]{4,3,2,1,0:T(8,128)S(1)} %copy-done, f32[2,3,8,1,256]{4,3,2,1,0:T(1,128)S(1)} %collective-permute-done.1, f32[2,3,8,65,256]{4,3,2,1,0:T(8,128)} %dynamic-update-slice.1, f32[64]{0:T(128)S(1)} %broadcast_multiply_fusion), kind=kLoop, calls=%fused_computation.49 | loop fusion | flops 3145728 | bytes 9486848 | tf_op jit(solution)/shard_map/mul | solution.py:482
  131.6 51.2 %all-to-all-done.in_ref = f32[16,3,2,64,256]{4,3,2,1,0:T(8,128)} async-done(((f32[16,3,2,64,256]{4,3,2,1,0:T(8,128)}), f32[16,3,2,64,256]{4,3,2,1,0:T(8,128)}, u32[]{:S(2)}, u32[]{:S(2)}) %all-to-all-start) | async-done | bytes 6291488 | tf_op jit(solution)/shard_map/all_to_all | solution.py:428
  182.9 6.0 %planes_to_layers.1 = f32[2,3,8,64,256]{4,3,2,1,0:T(8,128)} custom-call(f32[16,3,2,64,256]{4,3,2,1,0:T(8,128)} %all-to-all-done.in_ref), custom_call_target="tpu_custom_call" | custom-call | tf_op jit(solution)/shard_map/planes_to_layers/pallas_call | solution.py:430
  188.9 11.4 %multiply_reduce_fusion.9 = (f32[2,8,64,256]{3,2,1,0:T(8,128)}, f32[2,8,64,256]{3,2,1,0:T(8,128)}, f32[2,8,64,256]{3,2,1,0:T(8,128)}, f32[2,8,64,256]{3,2,1,0:T(...) fusion(f32[2,3,8,64,256]{4,3,2,1,0:T(8,128)S(1)} %copy-done, ...), kind=kLoop, calls=%fused_computation.41 | loop fusion | flops 17825790 | bytes 29933576 | tf_op jit(solution)/shard_map/reduce_sum | solution.py:52
  200.3 0.0 copy-start.2
  200.3 0.0 copy-start.3
  200.3 3.5 %subtract_bitcast_fusion = (f32[1,2,8,64,256]{4,3,2,1,0:T(8,128)S(1)}, f32[1,2,8,64,256]{4,3,2,1,0:T(8,128)S(1)}) fusion(f32[2,8,64,256,3]{3,2,1,4,0:T(8,128)} %get-tuple-element.34, f32[2,8,64,256,3]{3,2,1,0,4:T(8,128)} %bitcast.60), kind=kLoop, calls=%fused_computation.68 | loop fusion | flops 1572864 | bytes 8388608 | tf_op jit(solution)/shard_map/jit(cross)/sub | solution.py:50
  203.8 0.2 copy-done.2
  204.1 1.0 copy-done.3
  205.0 0.3 fusion.22
  205.3 0.0 copy-start.4
  205.3 0.4 fusion.10
  205.7 0.8 copy-done.4
  206.5 1.9 multiply_reduce_fusion.12
  208.5 0.1 copy.58
  208.6 8.2 %multiply_reduce_fusion.2 = (f32[2]{0:T(128)S(1)}, f32[2]{0:T(128)S(1)}, f32[2]{0:T(128)S(1)}, f32[2]{0:T(128)S(1)}, f32[2]{0:T(128)S(1)}, /*index=5*/f32[2,3,8,...) fusion(f32[2,3,8,64,256]{4,3,2,1,0:T(8,128)S(1)} %copy-done, ...), kind=kLoop, calls=%fused_computation.30 | loop fusion | flops 14155766 | bytes 25165864 | tf_op jit(solution)/shard_map/reduce_sum | solution.py:42
  216.8 0.1 copy.59
  216.9 0.1 copy.60
  217.0 0.1 copy.61
  217.1 0.1 copy.62
  217.2 0.1 copy.63
  217.3 0.1 copy.57
  217.4 0.1 stack.41
  217.5 48.4 %all-gather.1 = f32[32,2,7]{2,1,0:T(2,128)S(1)} all-gather(f32[1,2,7]{2,1,0:T(2,128)S(1)} %bitcast.69), channel_id=2, replica_groups=mesh['image'=8,'space'=4] {'image','space'}, dimensions={0}, use_global_device_ids=true | all-gather | bytes 1848 | tf_op jit(solution)/shard_map/all_gather | solution.py:514
  265.9 0.6 fusion.47
  266.5 1.4 select_select_fusion.1
  267.9 0.5 slice.221
  268.4 2.0 fusion.41
  270.5 0.1 copy.66
  270.5 0.1 copy.65
  270.6 0.1 copy.64
  270.7 0.1 constant_dynamic-slice_fusion
  270.8 0.5 multiply_bitcast_fusion
  271.3 7.0 %multiply_reduce_fusion.1 = (f32[2,8,64,256]{3,2,1,0:T(8,128)S(1)}, f32[2,3,8,64,256]{4,3,2,1,0:T(8,128)}) fusion(f32[2,3,8,64,256]{4,3,2,1,0:T(8,128)} %get-tuple-element.28, f32[2]{0:T(128)S(1)} %get-tuple-element.47, f32[2,3,8,64,256]{4,3,2,1,0:T(8,128)} %get-tuple-element.27, f32[2,3,8,64,256]{4,3,2,1,0:T(8,128)} %get-tuple-element.26, ...), kind=kLoop, calls=%fused_computation.28 | loop fusion | flops 5242880 | bytes 13631506 | tf_op jit(solution)/shard_map/reduce_sum | solution.py:548
  278.3 0.4 sqrt_reduce_fusion
  278.7 6.0 %pmax.7 = f32[2]{0:T(128)S(1)} all-reduce(f32[2]{0:T(128)S(1)} %sqrt_reduce_fusion), channel_id=1, replica_groups=mesh['image'=8,'space'=4] {'space'}, use_global_device_ids=true, to_apply=%region_15.16 | all-reduce | flops 2 | bytes 16 | tf_op jit(solution)/shard_map/pmax | solution.py:549
  284.7 0.0 copy-start.1
  284.7 3.0 %multiply_reduce_fusion = f32[2,8,64,256]{3,2,1,0:T(8,128)S(1)} fusion(f32[2,3,8,64,256]{4,3,2,1,0:T(8,128)S(1)} %copy-done, f32[2,3,8,64,256]{4,3,2,1,0:T(8,128)} %get-tuple-element.20, f32[2]{0:T(128)S(1)} %divide_minimum_fusion), kind=kLoop, calls=%fused_computation.26 | loop fusion | flops 2883584 | bytes 7340040 | tf_op jit(solution)/shard_map/reduce_sum | solution.py:552
  287.6 0.2 sqrt.29
  287.9 0.0 copy-done.1
  287.9 2.5 broadcast_divide_fusion
  (12 shorter events, 0.1 us)
Async XLA Ops:
  4.5 93.3 %collective-permute-start.2 = (f32[1,3,8,64,256]{4,3,2,1,0:T(8,128)}, f32[1,3,8,64,256]{4,3,2,1,0:T(8,128)}, u32[]{:S(2)}, u32[]{:S(2)}) collective-permute-start(f32[1,3,8,64,256]{4,3,2,1,0:T(8,128)} %get-tuple-element.38), channel_id=1, source_target_pairs={{0,4},{4,8},{8,12},{12,16},{16,20},{20,24},{24,28},{1,5},{5,9},{9,... | collective-permute-start | bytes 4718600 | tf_op jit(solution)/shard_map/ppermute | solution.py:28
  10.5 87.3 %collective-permute-start.3 = (f32[1,3,8,64,256]{4,3,2,1,0:T(8,128)}, f32[1,3,8,64,256]{4,3,2,1,0:T(8,128)}, u32[]{:S(2)}, u32[]{:S(2)}) collective-permute-start(f32[1,3,8,64,256]{4,3,2,1,0:T(8,128)} %get-tuple-element.39), channel_id=1, source_target_pairs={{4,0},{8,4},{12,8},{16,12},{20,16},{24,20},{28,24},{5,1},{9,5},{13... | collective-permute-start | bytes 4718600 | tf_op jit(solution)/shard_map/ppermute | solution.py:30
  17.4 80.4 %copy-start = (f32[2,3,8,64,256]{4,3,2,1,0:T(8,128)S(1)}, f32[2,3,8,64,256]{4,3,2,1,0:T(8,128)}, u32[]{:S(2)}) copy-start(f32[2,3,8,64,256]{4,3,2,1,0:T(8,128)} %in_ref.1) | copy-start | bytes 9437188
  103.2 79.7 %all-to-all-start = ((f32[16,3,2,64,256]{4,3,2,1,0:T(8,128)}), f32[16,3,2,64,256]{4,3,2,1,0:T(8,128)}, u32[]{:S(2)}, u32[]{:S(2)}) async-start(f32[16,3,2,64,256]{4,3,2,1,0:T(8,128)} %bitcast.62), calls=%async_computation | async-start | bytes 12582912 | tf_op jit(solution)/shard_map/all_to_all | solution.py:428
  113.3 11.9 %collective-permute-start = (f32[2,3,8,1,256]{4,3,2,1,0:T(1,128)S(1)}, f32[2,3,8,1,256]{4,3,2,1,0:T(1,128)S(1)}, u32[]{:S(2)}, u32[]{:S(2)}) collective-permute-start(f32[2,3,8,1,256]{4,3,2,1,0:T(1,128)S(1)} %get-tuple-element.36), channel_id=1, source_target_pairs={{1,0},{2,1},{3,2},{5,4},{6,5},{7,6},{9,8},{10,9},{11,10},{13,12},{... | collective-permute-start | bytes 147464 | tf_op jit(solution)/shard_map/ppermute | solution.py:30
  114.6 12.5 %collective-permute-start.1 = (f32[2,3,8,1,256]{4,3,2,1,0:T(1,128)S(1)}, f32[2,3,8,1,256]{4,3,2,1,0:T(1,128)S(1)}, u32[]{:S(2)}, u32[]{:S(2)}) collective-permute-start(f32[2,3,8,1,256]{4,3,2,1,0:T(1,128)S(1)} %get-tuple-element.37), channel_id=1, source_target_pairs={{0,1},{1,2},{2,3},{4,5},{5,6},{6,7},{8,9},{9,10},{10,11},{12,13},{... | collective-permute-start | bytes 147464 | tf_op jit(solution)/shard_map/ppermute | solution.py:28
  120.2 2.0 copy-start.5
  200.3 3.8 %copy-start.2 = (f32[2,3,8,64,256]{4,3,2,0,1:T(8,128)S(1)}, f32[2,3,8,64,256]{4,3,2,0,1:T(8,128)}, u32[]{:S(2)}) copy-start(f32[2,3,8,64,256]{4,3,2,0,1:T(8,128)} %copy.70) | copy-start | bytes 9437188
  200.3 4.7 %copy-start.3 = (f32[2,8,64,256,3]{3,2,1,4,0:T(8,128)S(1)}, f32[2,8,64,256,3]{3,2,1,4,0:T(8,128)}, u32[]{:S(2)}) copy-start(f32[2,8,64,256,3]{3,2,1,4,0:T(8,128)} %get-tuple-element.34) | copy-start | bytes 9437188
  205.3 1.2 copy-start.4
  284.7 3.2 %copy-start.1 = (f32[2,3,8,64,256]{4,3,2,1,0:T(8,128)S(1)}, f32[2,3,8,64,256]{4,3,2,1,0:T(8,128)}, u32[]{:S(2)}) copy-start(f32[2,3,8,64,256]{4,3,2,1,0:T(8,128)} %get-tuple-element.20) | copy-start | bytes 9437188

commit v3 on v2

--- a/solution.py
+++ b/solution.py
@@ -369,7 +369,74 @@
     lax.fori_loop(0, 6, backward, 0)
 
 
-def demag_pair(magnet, kernel, images, pair_index):
+def swap_kernel(shifts, combine, tile_ref, out_ref, held_ref, send_sem, recv_sem):
+    groups, images = lax.axis_size("space"), lax.axis_size("image")
+    me, image = lax.axis_index("space"), lax.axis_index("image")
+    routes = [
+        (n, shift, d)
+        for n, shift in enumerate(shifts)
+        for d in range(groups)
+        if shift != 0 or d != 0
+    ]
+
+    def target(shift, d):
+        return {"image": lax.rem(image - shift + images, images), "space": lax.rem(me + d, groups)}
+
+    barrier = pltpu.get_barrier_semaphore()
+    for n, shift, d in routes:
+        pl.semaphore_signal(
+            barrier, inc=1, device_id=target(shift, d), device_id_type=pl.DeviceIdType.MESH
+        )
+    pl.semaphore_wait(barrier, len(routes))
+
+    def copy_of(n, shift, d, slot):
+        return pltpu.make_async_remote_copy(
+            src_ref=tile_ref,
+            dst_ref=held_ref.at[n, slot],
+            send_sem=send_sem.at[n, d],
+            recv_sem=recv_sem.at[n, d],
+            device_id=target(shift, d),
+            device_id_type=pl.DeviceIdType.MESH,
+        )
+
+    for n, shift, d in routes:
+        copy_of(n, shift, d, me).start()
+    held_ref[shifts.index(0), me] = tile_ref[...]
+    for n, shift, d in routes:
+        copy_of(n, shift, d, lax.rem(me + groups - d, groups)).wait_recv()
+    for n in range(len(shifts)):
+        total = held_ref[n, 0]
+        for g in range(1, groups):
+            total = combine(total, held_ref[n, g])
+        out_ref[n] = total
+    for n, shift, d in routes:
+        copy_of(n, shift, d, me).wait_send()
+
+
+def swapped(values, shifts, combine, collective_id):
+    rows, columns = values.shape
+    tile = jnp.pad(values, ((0, -rows % 8), (0, -columns % 128)))
+    groups = lax.axis_size("space")
+    inside = pl.BlockSpec(memory_space=pltpu.VMEM)
+    result = pl.pallas_call(
+        functools.partial(swap_kernel, shifts, combine),
+        in_specs=[inside],
+        out_specs=inside,
+        out_shape=jax.ShapeDtypeStruct((len(shifts),) + tile.shape, jnp.float32),
+        scratch_shapes=[
+            pltpu.VMEM((len(shifts), groups) + tile.shape, jnp.float32),
+            pltpu.SemaphoreType.DMA((len(shifts), groups)),
+            pltpu.SemaphoreType.DMA((len(shifts), groups)),
+        ],
+        compiler_params=pltpu.CompilerParams(
+            collective_id=collective_id, has_side_effects=True
+        ),
+        name="swap_kernel",
+    )(tile)
+    return result[:, :rows, :columns]
+
+
+def demag_pair(magnet, kernel, images, early_work, pair_index):
     layer_count, row_count, column_count = magnet.shape[2:]
     groups = lax.axis_size("space")
     local_planes = 2 * layer_count // groups
@@ -426,6 +493,7 @@
     planes = planes.reshape(plane_dims)
     planes, *images = lax.optimization_barrier((planes, *images))
     planes = lax.all_to_all(planes, "space", split_axis=0, concat_axis=0, tiled=True)
+    planes, early = lax.optimization_barrier((planes, early_work(images)))
     padded_cells = 8 * layer_count * full_rows * column_count
     field = pl.pallas_call(
         functools.partial(planes_to_layers, -1.0 / padded_cells),
@@ -435,15 +503,17 @@
         out_shape=jax.ShapeDtypeStruct(magnet.shape, jnp.float32),
         name="planes_to_layers",
     )(planes)
-    return field, images
-
-
-def demag_field(magnet, kernel, images):
+    return field, images, early
+
+
+def demag_field(magnet, kernel, images, early_work):
     fields = []
     for index, start in enumerate(range(0, magnet.shape[0], 2)):
-        field, images = demag_pair(magnet[start : start + 2], kernel, images, index)
+        field, images, early = demag_pair(
+            magnet[start : start + 2], kernel, images, early_work, index
+        )
         fields.append(field)
-    return (fields[0] if len(fields) == 1 else jnp.concatenate(fields, axis=0)), images
+    return (fields[0] if len(fields) == 1 else jnp.concatenate(fields, axis=0)), images, early
 
 
 def local_fields(magnet, anisotropy):
@@ -491,8 +561,21 @@
     image_count = magnet.shape[0]
     cell_count = magnet.shape[2] * magnet.shape[3] * lax.axis_size("space") * magnet.shape[4]
     framed = extended(magnet, (("image", 0),), 1)
-    demag, (framed,) = demag_field(magnet, kernel, [framed])
-    fields = local_fields(magnet, anisotropy) + demag
+
+    def early_work(images):
+        prior, following = images[0][:-2], images[0][2:]
+        ahead = project(following - magnet, magnet)
+        behind = project(magnet - prior, magnet)
+        return (
+            local_fields(magnet, anisotropy),
+            total_cells(angle_squared(magnet, following)),
+            total_cells(ahead * ahead),
+            total_cells(ahead * behind),
+            total_cells(behind * behind),
+        )
+
+    demag, (framed,), early = demag_field(magnet, kernel, [framed], early_work)
+    fields = early[0] + demag
     prior_image = framed[:-2]
     next_image = framed[2:]
     true_force = project(fields, magnet)
@@ -501,21 +584,15 @@
     sums = jnp.stack(
         [
             -0.5 * total_cells(magnet * fields),
-            total_cells(angle_squared(magnet, next_image)),
-            total_cells(tangent_next * tangent_next),
-            total_cells(tangent_next * tangent_prior),
-            total_cells(tangent_prior * tangent_prior),
+            *early[1:],
             total_cells(true_force * tangent_next),
             total_cells(true_force * tangent_prior),
         ],
         axis=1,
     )
     band_size = image_count * lax.axis_size("image")
-    gathered = lax.all_gather(sums, ("image", "space"))
-    gathered = gathered.reshape(
-        (lax.axis_size("image"), lax.axis_size("space")) + sums.shape
-    )
-    band = jnp.sum(gathered, axis=1).reshape(band_size, sums.shape[1])
+    swaps = swapped(sums, (-1, 0, 1), jnp.add, 64)
+    band = jnp.concatenate([swaps[0, -1:], swaps[1], swaps[2, :1]], axis=0)
     energy_band, distance_band = band[:, 0], jnp.sqrt(band[:, 1] / cell_count)
     weight_next, weight_prior = tangent_weights(
         energy_band, jnp.roll(energy_band, -1), jnp.roll(energy_band, 1)
@@ -529,16 +606,11 @@
     tangent_scale = jnp.sqrt(jnp.maximum(length_squares, 0.0) / cell_count + epsilon)
     parallel = drive_total / (cell_count * tangent_scale)
     spring = spring_strength * (distance_band - jnp.roll(distance_band, 1))
-    image_index = jnp.arange(band_size)
+    first_image = lax.axis_index("image") * image_count
+    image_index = first_image - 1 + jnp.arange(image_count + 2)
     interior = ((image_index > 0) & (image_index < band_size - 1)).astype(jnp.float32)
     pull = (spring - parallel) / tangent_scale
-    first_image = lax.axis_index("image") * image_count
-    mine = lax.dynamic_slice_in_dim(
-        jnp.stack([energy_band, pull * weight_next, pull * weight_prior, interior], axis=1),
-        first_image,
-        image_count,
-        axis=0,
-    )
+    mine = jnp.stack([energy_band, pull * weight_next, pull * weight_prior, interior], axis=1)[1:-1]
     energy_total = mine[:, 0]
     band_force = jnp.where(
         lift_axes(mine[:, 3]) > 0.0,
@@ -546,7 +618,7 @@
         0.0,
     )
     local_largest = jnp.max(jnp.sqrt(jnp.sum(band_force * band_force, axis=1)), axis=(1, 2, 3))
-    largest = lax.pmax(local_largest, "space")
+    largest = swapped(local_largest[None, :], (0,), jnp.maximum, 65)[0, 0]
     move_scale = jnp.minimum(step_limit, rotation_limit / (largest + epsilon))
     stepped = magnet + lift_axes(move_scale) * band_force
     updated = stepped / jnp.sqrt(jnp.sum(stepped * stepped, axis=1, keepdims=True))

time: 291 us -> 261 us (0.90)
  blocking collectives: 54.4 us -> 0 us
  Pallas kernels: 91.9 us -> 136 us
  waiting for transfers between devices: 51.2 us -> 29.3 us
    all_gather x1 -> x0, blocking collectives: 48.4 us -> none  [body(): gathered = lax.all_gather(sums, ('image', 'space'))]
    pallas_call x0 -> x2, Pallas kernels: none -> 43.9 us  [swapped(): pl.pallas_call(functools.partial(swap_kernel, shifts, combine), in_specs=...]
    all_to_all x1, waiting for transfers between devices: 51.2 us -> 29.3 us  [demag_pair(): lax.all_to_all(planes, 'space', split_axis=0, concat_axis=0, tiled=True)]
    pmax x1 -> x0, blocking collectives: 5.96 us -> none  [body(): largest = lax.pmax(local_largest, 'space')]
    reduce_sum x2 -> x4, other arithmetic: 10.2 us -> 13.5 us  [total_cells(): return jnp.sum(values, axis=tuple(range(1, values.ndim)))]
    reduce_sum x2 -> x1, other arithmetic: 11.5 us -> 11.1 us  [project(): return vector - jnp.sum(vector * magnet, axis=1, keepdims=True) * magnet]
    unnamed x14 -> x26, local copies, waits for them, and re-layouts: 6.09 us -> 6.05 us
  transfers between devices with their start and end apart: 5 -> 5, of which waited for: 1 -> 1; matrix products, arithmetic and copies ran while one was open for 4% -> 12% of each run, Pallas kernels for 30% -> 33%
where the time goes in v3:
time: 261 us; the launch traced here: 260 us
  Pallas kernels  136 us (52%)
  other arithmetic  53.5 us (20%)
  waiting for transfers between devices  29.3 us (11%)
  starting transfers between devices  24.5 us (9%)
  local copies, waits for them, and re-layouts  16.3 us (6%)
    pallas_call x1, Pallas kernels, demag_pair(): pl.pallas_call(plane_kernel, in_specs=[anywhere, anywhere] + [inside] * l...  80.4 us
    pallas_call x2, Pallas kernels, swapped(): pl.pallas_call(functools.partial(swap_kernel, shifts, combine), in_specs=...  43.9 us
    all_to_all x1, waiting for transfers between devices, demag_pair(): lax.all_to_all(planes, 'space', split_axis=0, concat_axis=0, tiled=True)  29.3 us
    reduce_sum x4, other arithmetic, total_cells(): return jnp.sum(values, axis=tuple(range(1, values.ndim)))  13.5 us
    ppermute x2, starting transfers between devices, extended(): lax.ppermute(tail, axis, [(i, (i + 1) % count) for i in range(ends)])  11.7 us
    reduce_sum x1, other arithmetic, project(): return vector - jnp.sum(vector * magnet, axis=1, keepdims=True) * magnet  11.1 us
    all_to_all x1, starting transfers between devices, demag_pair(): lax.all_to_all(planes, 'space', split_axis=0, concat_axis=0, tiled=True)  10.2 us
    reduce_sum x1, other arithmetic, body(): jnp.sum(band_force * band_force, axis=1)  7.01 us
  transfers between devices with their start and end apart: 5, of which 1 were waited for; matrix products, arithmetic and copies ran while one was open for 12% of the time, Pallas kernels for 33%

profile of v3, /device:TPU:0, one launch (start us, length us, event | category | flops | bytes accessed | tf_op | source)
XLA Modules:
  0.0 260.3 jit_solution(14017847600924540845)
XLA Ops:
  0.6 3.9 %fusion.33 = (f32[1,3,8,64,256]{4,3,2,1,0:T(8,128)}, f32[1,3,8,64,256]{4,3,2,1,0:T(8,128)}) fusion(f32[2,3,8,64,256]{4,3,2,1,0:T(8,128)} %in_ref.1), kind=kLoop, calls=%fused_computation.111 | loop fusion | bytes 6291456 | tf_op jit(solution)/shard_map/slice | solution.py:25
  4.5 6.0 %collective-permute-start = (f32[1,3,8,64,256]{4,3,2,1,0:T(8,128)}, f32[1,3,8,64,256]{4,3,2,1,0:T(8,128)}, u32[]{:S(2)}, u32[]{:S(2)}) collective-permute-start(f32[1,3,8,64,256]{4,3,2,1,0:T(8,128)} %get-tuple-element.49), channel_id=1, source_target_pairs={{0,4},{4,8},{8,12},{12,16},{16,20},{20,24},{24,28},{1,5},{5,9},{9,... | collective-permute-start | bytes 4718600 | tf_op jit(solution)/shard_map/ppermute | solution.py:28
  10.6 1.3 collective-permute-start.1
  11.9 5.5 %layers_to_planes.1 = f32[16,3,2,64,256]{4,3,2,1,0:T(8,128)} custom-call(f32[2,3,8,64,256]{4,3,2,1,0:T(8,128)} %in_ref.1), custom_call_target="tpu_custom_call" | custom-call | tf_op jit(solution)/shard_map/layers_to_planes/pallas_call | solution.py:447
  17.4 80.4 %plane_kernel.1 = f32[4,4,3,2,64,256]{5,4,3,2,1,0:T(8,128)} custom-call(f32[4,4,3,2,64,256]{5,4,3,2,1,0:T(8,128)} %bitcast.68, f32[6,4,512,512]{3,2,1,0:T(8,128)} %kernel_ref.1, bf16[2,256,512]{2,1,0:T(8,128)(2,1)} %constant.71.clone.fy_ref, bf16[2,512,256]{2,1,0:T(8,128)(2,1)} %constant.72.clone.fx_ref, bf16[2,256,512]{2,1,0:T(8,128)(2,1)} %constant.73.clone.gx_ref, ...), custom_call_target="tpu_custom_call" | custom-call | flops 28991029248 | bytes 25165824 | tf_op jit(solution)/shard_map/plane_kernel/pallas_call | solution.py:469
  97.8 0.0 collective-permute-done
  97.8 0.0 collective-permute-done.1
  97.8 0.0 copy-done
  97.8 5.3 %pad_maximum_fusion = f32[4,3,8,64,256]{4,3,2,1,0:T(8,128)} fusion(f32[1,3,8,64,256]{4,3,2,1,0:T(8,128)} %collective-permute-done.1, f32[2,3,8,64,256]{4,3,2,1,0:T(8,128)S(1)} %copy-done, f32[1,3,8,64,256]{4,3,2,1,0:T(8,128)} %collective-permute-done), kind=kLoop, calls=%fused_computation.8 | loop fusion | flops 3145728 | bytes 12582912 | tf_op jit(solution)/shard_map/concatenate | solution.py:26
  103.1 10.2 %all-to-all-start = ((f32[16,3,2,64,256]{4,3,2,1,0:T(8,128)}), f32[16,3,2,64,256]{4,3,2,1,0:T(8,128)}, u32[]{:S(2)}, u32[]{:S(2)}) async-start(f32[16,3,2,64,256]{4,3,2,1,0:T(8,128)} %bitcast.67), calls=%async_computation | async-start | bytes 12582912 | tf_op jit(solution)/shard_map/all_to_all | solution.py:495
  113.3 0.1 fusion.32
  113.4 1.3 collective-permute-start.2
  114.7 5.6 %collective-permute-start.3 = (f32[2,3,8,1,256]{4,3,2,1,0:T(1,128)S(1)}, f32[2,3,8,1,256]{4,3,2,1,0:T(1,128)S(1)}, u32[]{:S(2)}, u32[]{:S(2)}) collective-permute-start(f32[2,3,8,1,256]{4,3,2,1,0:T(1,128)S(1)} %get-tuple-element.48), channel_id=1, source_target_pairs={{0,1},{1,2},{2,3},{4,5},{5,6},{6,7},{8,9},{9,10},{10,11},{12,13},{... | collective-permute-start | bytes 147464 | tf_op jit(solution)/shard_map/ppermute | solution.py:28
  120.4 0.0 copy-done.9
  120.4 0.1 compare_bitcast_fusion
  120.5 1.0 add_subtract_fusion
  121.4 2.0 constant_dynamic-update-slice_fusion
  123.4 2.0 copy.76
  125.5 0.0 collective-permute-done.2
  125.5 1.9 dynamic-update-slice.1
  127.4 0.0 collective-permute-done.3
  127.4 4.5 %fusion.12 = (f32[2,1,8,64,256]{4,3,2,1,0:T(8,128)}, f32[2,1,8,64,256]{4,3,2,1,0:T(8,128)}, f32[2,1,8,64,256]{4,3,2,1,0:T(8,128)}) fusion(f32[2,3,8,64,256]{4,3,2,1,0:T(8,128)S(1)} %copy-done, f32[2,3,8,1,256]{4,3,2,1,0:T(1,128)S(1)} %collective-permute-done.3, f32[2,3,8,65,256]{4,3,2,1,0:T(8,128)} %dynamic-update-slice.1, f32[64]{0:T(128)S(1)} %broadcast_multiply_fusion), kind=kLoop, calls=%fused_computation.48 | loop fusion | flops 3145728 | bytes 9486848 | tf_op jit(solution)/shard_map/mul | solution.py:552
  131.9 11.1 %multiply_reduce_fusion.8 = (f32[2,8,64,256]{3,2,1,0:T(8,128)}, f32[2,8,64,256]{3,2,1,0:T(8,128)}, f32[2,8,64,256]{3,2,1,0:T(8,128)}, f32[2,8,64,256,3]{3,2,1,4,0:T(8,128)}, f32[2,3,8,64,256]{4,3,2,1,0:T(8,128)}) fusion(f32[2,3,8,64,256]{4,3,2,1,0:T(8,128)S(1)} %copy-done, f32[4,3,8,64,256]{4,3,2,1,0:T(8,128)} %pad_maximum_fusion, ...), kind=kLoop, calls=%fused_computation.39 | loop fusion | flops 14942208 | bytes 25739264 | tf_op jit(solution)/shard_map/reduce_sum | solution.py:46
  143.0 0.0 copy-done.4
  143.0 2.0 fusion.21
  145.0 0.5 copy-done.5
  145.6 0.6 subtract_bitcast_fusion
  146.2 0.3 fusion.9
  146.6 1.1 copy-done.6
  147.6 1.9 multiply_reduce_fusion.12
  149.6 0.0 copy-done.7
  149.6 4.1 %multiply_reduce_fusion.4 = (f32[2]{0:T(128)S(1)}, f32[2]{0:T(128)S(1)}, f32[2]{0:T(128)S(1)}, f32[2,3,8,64,256]{4,3,2,1,0:T(8,128)}, f32[2,3,8,64,256]{4,3,2,1,0:T(8,128)}) fusion(f32[2,3,8,64,256]{4,3,2,1,0:T(8,128)S(1)} %copy-done, f32[2,8,64,256]{3,2,1,0:T(8,128)S(1)} %copy-done.7, f32[4,3,8,64,256]{4,3,2,1,0:T(8,128)S(1)} %bitcast.64, ...), kind=kLoop, calls=%fused_computation.32 | loop fusion | flops 9437178 | bytes 17825816 | tf_op jit(solution)/shard_map/reduce_sum | solution.py:42
  153.7 29.3 %all-to-all-done.in_ref = f32[16,3,2,64,256]{4,3,2,1,0:T(8,128)} async-done(((f32[16,3,2,64,256]{4,3,2,1,0:T(8,128)}), f32[16,3,2,64,256]{4,3,2,1,0:T(8,128)}, u32[]{:S(2)}, u32[]{:S(2)}) %all-to-all-start) | async-done | bytes 6291488 | tf_op jit(solution)/shard_map/all_to_all | solution.py:495
  183.0 6.0 %planes_to_layers.1 = f32[2,3,8,64,256]{4,3,2,1,0:T(8,128)} custom-call(f32[16,3,2,64,256]{4,3,2,1,0:T(8,128)} %all-to-all-done.in_ref), custom_call_target="tpu_custom_call" | custom-call | tf_op jit(solution)/shard_map/planes_to_layers/pallas_call | solution.py:498
  189.0 4.3 %multiply_reduce_fusion.10 = (f32[2]{0:T(128)S(1)}, f32[2,8,64,256]{3,2,1,0:T(8,128)S(1)}, f32[2,3,8,64,256]{4,3,2,1,0:T(8,128)S(1)}) fusion(f32[2,3,8,64,256]{4,3,2,1,0:T(8,128)S(1)} %copy-done, f32[2,3,8,64,256]{4,3,2,1,0:T(8,128)} %get-tuple-element.13, f32[2,3,8,64,256]{4,3,2,1,0:T(8,128)} %planes_to_layers.1), kind=kLoop, calls=%fused_computation.44 | loop fusion | flops 2883582 | bytes 13631496 | tf_op jit(solution)/shard_map/reduce_sum | solution.py:42
  193.3 0.0 copy-done.1
  193.4 0.4 copy-done.2
  193.7 3.1 %multiply_reduce_fusion.2 = (f32[2]{0:T(128)S(1)}, f32[2]{0:T(128)S(1)}, f32[2,3,8,64,256]{4,3,2,1,0:T(8,128)}) fusion(f32[2,3,8,64,256]{4,3,2,1,0:T(8,128)S(1)} %copy-done.2, f32[2,3,8,64,256]{4,3,2,1,0:T(8,128)S(1)} %copy-done.1, f32[2,3,8,64,256]{4,3,2,1,0:T(8,128)S(1)} %get-tuple-element.37, f32[2,3,8,64,256]{4,3,2,1,0:T(8,128)S(1)} %copy-done, ...), kind=kLoop, calls=%fused_computation.29 | loop fusion | flops 4718588 | bytes 16777232 | tf_op jit(solution)/shard_map/reduce_sum | solution.py:42
  196.9 0.1 copy.71
  197.0 0.1 copy.72
  197.1 0.1 copy.66
  197.1 0.1 copy.67
  197.2 0.1 copy.68
  197.3 0.1 copy.69
  197.4 0.1 copy.70
  197.5 0.1 stack.39
  197.6 0.6 pad.13.tile_ref
  198.2 38.9 %swap_kernel.2 = f32[3,8,128]{2,1,0:T(8,128)} custom-call(f32[8,128]{1,0:T(8,128)} %pad.13.tile_ref), custom_call_target="tpu_custom_call" | custom-call | tf_op jit(solution)/shard_map/swap_kernel/pallas_call | solution.py:421
  237.2 0.7 slice_bitcast_fusion.5
  237.8 0.7 slice_bitcast_fusion.3
  238.6 0.6 multiply_reduce_fusion.13
  239.2 0.1 select_select_fusion.1
  239.3 0.6 slice.231
  239.9 0.8 fusion.29
  240.7 0.1 slice_reduce_fusion
  240.8 0.1 slice_reduce_fusion.1
  240.9 7.0 %multiply_reduce_fusion.1 = (f32[2,8,64,256]{3,2,1,0:T(8,128)S(1)}, f32[2,3,8,64,256]{4,3,2,1,0:T(8,128)}) fusion(f32[2,3,8,64,256]{4,3,2,1,0:T(8,128)} %get-tuple-element.39, f32[2]{0:T(128)S(1)} %slice_reduce_fusion, f32[2,3,8,64,256]{4,3,2,1,0:T(8,128)} %get-tuple-element.36, f32[2,3,8,64,256]{4,3,2,1,0:T(8,128)} %get-tuple-element.38, ...), kind=kLoop, calls=%fused_computation.27 | loop fusion | flops 5242880 | bytes 13631506 | tf_op jit(solution)/shard_map/reduce_sum | solution.py:620
  247.9 0.4 sqrt_reduce_fusion
  248.3 0.6 pad.14.tile_ref
  248.9 5.0 %swap_kernel.3 = f32[1,8,128]{2,1,0:T(8,128)} custom-call(f32[8,128]{1,0:T(8,128)} %pad.14.tile_ref), custom_call_target="tpu_custom_call" | custom-call | tf_op jit(solution)/shard_map/swap_kernel/pallas_call | solution.py:421
  253.9 0.7 minimum_bitcast_fusion
  254.6 3.0 %multiply_reduce_fusion = f32[2,8,64,256]{3,2,1,0:T(8,128)S(1)} fusion(f32[2,3,8,64,256]{4,3,2,1,0:T(8,128)S(1)} %copy-done, f32[2,3,8,64,256]{4,3,2,1,0:T(8,128)} %get-tuple-element.30, f32[2]{0:T(128)S(1)} %minimum_bitcast_fusion), kind=kLoop, calls=%fused_computation.25 | loop fusion | flops 2883584 | bytes 7340040 | tf_op jit(solution)/shard_map/reduce_sum | solution.py:624
  257.5 0.2 sqrt.29
  257.8 2.5 broadcast_divide_fusion
  (26 shorter events, 0.1 us)
Async XLA Ops:
  4.5 93.2 %collective-permute-start = (f32[1,3,8,64,256]{4,3,2,1,0:T(8,128)}, f32[1,3,8,64,256]{4,3,2,1,0:T(8,128)}, u32[]{:S(2)}, u32[]{:S(2)}) collective-permute-start(f32[1,3,8,64,256]{4,3,2,1,0:T(8,128)} %get-tuple-element.49), channel_id=1, source_target_pairs={{0,4},{4,8},{8,12},{12,16},{16,20},{20,24},{24,28},{1,5},{5,9},{9,... | collective-permute-start | bytes 4718600 | tf_op jit(solution)/shard_map/ppermute | solution.py:28
  10.6 87.2 %collective-permute-start.1 = (f32[1,3,8,64,256]{4,3,2,1,0:T(8,128)}, f32[1,3,8,64,256]{4,3,2,1,0:T(8,128)}, u32[]{:S(2)}, u32[]{:S(2)}) collective-permute-start(f32[1,3,8,64,256]{4,3,2,1,0:T(8,128)} %get-tuple-element.50), channel_id=1, source_target_pairs={{4,0},{8,4},{12,8},{16,12},{20,16},{24,20},{28,24},{5,1},{9,5},{13... | collective-permute-start | bytes 4718600 | tf_op jit(solution)/shard_map/ppermute | solution.py:30
  17.4 80.4 %copy-start = (f32[2,3,8,64,256]{4,3,2,1,0:T(8,128)S(1)}, f32[2,3,8,64,256]{4,3,2,1,0:T(8,128)}, u32[]{:S(2)}) copy-start(f32[2,3,8,64,256]{4,3,2,1,0:T(8,128)} %in_ref.1) | copy-start | bytes 9437188
  103.1 17.3 %copy-start.9 = (f32[64]{0:T(128)S(1)}, f32[64]{0:T(128)}, u32[]{:S(2)}) copy-start(f32[64]{0:T(128)} %param.8) | copy-start | bytes 772
  103.1 79.9 %all-to-all-start = ((f32[16,3,2,64,256]{4,3,2,1,0:T(8,128)}), f32[16,3,2,64,256]{4,3,2,1,0:T(8,128)}, u32[]{:S(2)}, u32[]{:S(2)}) async-start(f32[16,3,2,64,256]{4,3,2,1,0:T(8,128)} %bitcast.67), calls=%async_computation | async-start | bytes 12582912 | tf_op jit(solution)/shard_map/all_to_all | solution.py:495
  113.4 12.1 %collective-permute-start.2 = (f32[2,3,8,1,256]{4,3,2,1,0:T(1,128)S(1)}, f32[2,3,8,1,256]{4,3,2,1,0:T(1,128)S(1)}, u32[]{:S(2)}, u32[]{:S(2)}) collective-permute-start(f32[2,3,8,1,256]{4,3,2,1,0:T(1,128)S(1)} %get-tuple-element.47), channel_id=1, source_target_pairs={{1,0},{2,1},{3,2},{5,4},{6,5},{7,6},{9,8},{10,9},{11,10},{13,12},{... | collective-permute-start | bytes 147464 | tf_op jit(solution)/shard_map/ppermute | solution.py:30
  114.7 12.7 %collective-permute-start.3 = (f32[2,3,8,1,256]{4,3,2,1,0:T(1,128)S(1)}, f32[2,3,8,1,256]{4,3,2,1,0:T(1,128)S(1)}, u32[]{:S(2)}, u32[]{:S(2)}) collective-permute-start(f32[2,3,8,1,256]{4,3,2,1,0:T(1,128)S(1)} %get-tuple-element.48), channel_id=1, source_target_pairs={{0,1},{1,2},{2,3},{4,5},{5,6},{6,7},{8,9},{9,10},{10,11},{12,13},{... | collective-permute-start | bytes 147464 | tf_op jit(solution)/shard_map/ppermute | solution.py:28
  131.9 11.1 %copy-start.4 = (f32[2,3,8,64,256]{4,3,2,0,1:T(8,128)S(1)}, f32[2,3,8,64,256]{4,3,2,0,1:T(8,128)}, u32[]{:S(2)}) copy-start(f32[2,3,8,64,256]{4,3,2,0,1:T(8,128)} %copy.76) | copy-start | bytes 9437188
  143.0 2.5 copy-start.5
  143.0 6.5 %slice-start = ((s8[6291456]{0:T(1024)(128)(4,1)}), s8[4194304]{0:T(1024)(128)(4,1)S(1)}, s32[]{:S(2)}) async-start(s8[6291456]{0:T(1024)(128)(4,1)} %bitcast.63), calls=%async_computation.1 | async-start | bytes 8388608
  145.6 4.0 %slice-start.1 = ((s8[6291456]{0:T(1024)(128)(4,1)}), s8[2097152]{0:T(1024)(128)(4,1)S(1)}, s32[]{:S(2)}) async-start(s8[6291456]{0:T(1024)(128)(4,1)} %bitcast.63), calls=%async_computation.2 | async-start | bytes 4194304
  146.2 1.4 copy-start.6
  146.2 3.4 %copy-start.7 = (f32[2,8,64,256]{3,2,1,0:T(8,128)S(1)}, f32[2,8,64,256]{3,2,1,0:T(8,128)}, u32[]{:S(2)}) copy-start(f32[2,8,64,256]{3,2,1,0:T(8,128)} %get-tuple-element.19) | copy-start | bytes 3145732
  146.2 3.4 %copy-start.8 = (f32[2,8,64,256]{3,2,1,0:T(8,128)S(1)}, f32[2,8,64,256]{3,2,1,0:T(8,128)}, u32[]{:S(2)}) copy-start(f32[2,8,64,256]{3,2,1,0:T(8,128)} %get-tuple-element.20) | copy-start | bytes 3145732
  189.0 4.3 %copy-start.1 = (f32[2,3,8,64,256]{4,3,2,1,0:T(8,128)S(1)}, f32[2,3,8,64,256]{4,3,2,1,0:T(8,128)}, u32[]{:S(2)}) copy-start(f32[2,3,8,64,256]{4,3,2,1,0:T(8,128)} %get-tuple-element.38) | copy-start | bytes 9437188
  189.0 4.7 %copy-start.2 = (f32[2,3,8,64,256]{4,3,2,1,0:T(8,128)S(1)}, f32[2,3,8,64,256]{4,3,2,1,0:T(8,128)}, u32[]{:S(2)}) copy-start(f32[2,3,8,64,256]{4,3,2,1,0:T(8,128)} %get-tuple-element.39) | copy-start | bytes 9437188
  254.6 3.2 %copy-start.3 = (f32[2,3,8,64,256]{4,3,2,1,0:T(8,128)S(1)}, f32[2,3,8,64,256]{4,3,2,1,0:T(8,128)}, u32[]{:S(2)}) copy-start(f32[2,3,8,64,256]{4,3,2,1,0:T(8,128)} %get-tuple-element.30) | copy-start | bytes 9437188

commit v4 on v3

--- a/solution.py
+++ b/solution.py
@@ -516,11 +516,10 @@
     return (fields[0] if len(fields) == 1 else jnp.concatenate(fields, axis=0)), images, early
 
 
-def local_fields(magnet, anisotropy):
+def local_fields(magnet, anisotropy, rimmed):
     layer_count = magnet.shape[2]
     row_count = magnet.shape[3]
     column_count = magnet.shape[4]
-    rimmed = extended(magnet, (("space", 3),), 1)
     x_plus = rimmed[:, :, :, 2:]
     x_minus = rimmed[:, :, :, :-2]
     padded = jnp.pad(magnet, ((0, 0), (0, 0), (1, 1), (0, 0), (1, 1)))
@@ -561,20 +560,21 @@
     image_count = magnet.shape[0]
     cell_count = magnet.shape[2] * magnet.shape[3] * lax.axis_size("space") * magnet.shape[4]
     framed = extended(magnet, (("image", 0),), 1)
+    rimmed = extended(magnet, (("space", 3),), 1)
 
     def early_work(images):
         prior, following = images[0][:-2], images[0][2:]
         ahead = project(following - magnet, magnet)
         behind = project(magnet - prior, magnet)
         return (
-            local_fields(magnet, anisotropy),
+            local_fields(magnet, anisotropy, images[1]),
             total_cells(angle_squared(magnet, following)),
             total_cells(ahead * ahead),
             total_cells(ahead * behind),
             total_cells(behind * behind),
         )
 
-    demag, (framed,), early = demag_field(magnet, kernel, [framed], early_work)
+    demag, (framed, _), early = demag_field(magnet, kernel, [framed, rimmed], early_work)
     fields = early[0] + demag
     prior_image = framed[:-2]
     next_image = framed[2:]

time: 261 us -> 242 us (0.927)
  Pallas kernels: 136 us -> 111 us
  waiting for transfers between devices: 29.3 us -> 37.1 us
  other arithmetic: 53.5 us -> 59.1 us
  starting transfers between devices: 24.5 us -> 20.7 us
  local copies, waits for them, and re-layouts: 16.3 us -> 13.3 us
    pallas_call x2, Pallas kernels: 43.9 us -> 16.4 us  [swapped(): pl.pallas_call(functools.partial(swap_kernel, shifts, combine), in_specs=...]
    all_to_all x1, waiting for transfers between devices: 29.3 us -> 37.1 us  [demag_pair(): lax.all_to_all(planes, 'space', split_axis=0, concat_axis=0, tiled=True)]
    ppermute x2, starting transfers between devices: 11.7 us -> 7.55 us  [extended(): lax.ppermute(tail, axis, [(i, (i + 1) % count) for i in range(ends)])]
    sub x2, other arithmetic: 2.62 us -> 5.45 us  [angle_squared(): normal_part = jnp.cross(first, second, axis=1)]
    concatenate x1 -> x2, other arithmetic: 5.3 us -> 7.65 us  [extended(): jnp.concatenate([lax.ppermute(tail, axis, [(i, (i + 1) % count) for i in...]
    unnamed x26 -> x25, local copies, waits for them, and re-layouts: 6.05 us -> 3.81 us
  transfers between devices with their start and end apart: 5 -> 5, of which waited for: 1 -> 1; matrix products, arithmetic and copies ran while one was open for 12% -> 14% of each run, Pallas kernels for 33% -> 36%
where the time goes in v4:
time: 242 us
  Pallas kernels  111 us (46%)
  other arithmetic  59.1 us (24%)
  waiting for transfers between devices  37.1 us (15%)
  starting transfers between devices  20.7 us (9%)
  local copies, waits for them, and re-layouts  13.3 us (5%)
    pallas_call x1, Pallas kernels, demag_pair(): pl.pallas_call(plane_kernel, in_specs=[anywhere, anywhere] + [inside] * l...  82.7 us
    all_to_all x1, waiting for transfers between devices, demag_pair(): lax.all_to_all(planes, 'space', split_axis=0, concat_axis=0, tiled=True)  37.1 us
    pallas_call x2, Pallas kernels, swapped(): pl.pallas_call(functools.partial(swap_kernel, shifts, combine), in_specs=...  16.4 us
    reduce_sum x4, other arithmetic, total_cells(): return jnp.sum(values, axis=tuple(range(1, values.ndim)))  13.5 us
    reduce_sum x1, other arithmetic, project(): return vector - jnp.sum(vector * magnet, axis=1, keepdims=True) * magnet  10.6 us
    all_to_all x1, starting transfers between devices, demag_pair(): lax.all_to_all(planes, 'space', split_axis=0, concat_axis=0, tiled=True)  10.6 us
    concatenate x2, other arithmetic, extended(): jnp.concatenate([lax.ppermute(tail, axis, [(i, (i + 1) % count) for i in...  7.65 us
    ppermute x2, starting transfers between devices, extended(): lax.ppermute(tail, axis, [(i, (i + 1) % count) for i in range(ends)])  7.55 us
  transfers between devices with their start and end apart: 5, of which 1 were waited for; matrix products, arithmetic and copies ran while one was open for 14% of the time, Pallas kernels for 36%

profile of v4, /device:TPU:0, one launch (start us, length us, event | category | flops | bytes accessed | tf_op | source)
XLA Modules:
  0.0 241.7 jit_solution(2187860699596797588)
XLA Ops:
  0.6 3.9 %fusion.27 = (f32[1,3,8,64,256]{4,3,2,1,0:T(8,128)}, f32[1,3,8,64,256]{4,3,2,1,0:T(8,128)}) fusion(f32[2,3,8,64,256]{4,3,2,1,0:T(8,128)} %in_ref.1), kind=kLoop, calls=%fused_computation.101 | loop fusion | bytes 6291456 | tf_op jit(solution)/shard_map/slice | solution.py:25
  4.5 6.1 %collective-permute-start = (f32[1,3,8,64,256]{4,3,2,1,0:T(8,128)}, f32[1,3,8,64,256]{4,3,2,1,0:T(8,128)}, u32[]{:S(2)}, u32[]{:S(2)}) collective-permute-start(f32[1,3,8,64,256]{4,3,2,1,0:T(8,128)} %get-tuple-element.51), channel_id=1, source_target_pairs={{0,4},{4,8},{8,12},{12,16},{16,20},{20,24},{24,28},{1,5},{5,9},{9,... | collective-permute-start | bytes 4718600 | tf_op jit(solution)/shard_map/ppermute | solution.py:28
  10.6 1.3 collective-permute-start.1
  11.9 1.2 fusion.26
  13.1 1.5 collective-permute-start.2
  14.6 1.3 collective-permute-start.3
  15.9 5.5 %layers_to_planes.1 = f32[16,3,2,64,256]{4,3,2,1,0:T(8,128)} custom-call(f32[2,3,8,64,256]{4,3,2,1,0:T(8,128)} %in_ref.1), custom_call_target="tpu_custom_call" | custom-call | tf_op jit(solution)/shard_map/layers_to_planes/pallas_call | solution.py:447
  21.4 82.7 %plane_kernel.1 = f32[4,4,3,2,64,256]{5,4,3,2,1,0:T(8,128)} custom-call(f32[4,4,3,2,64,256]{5,4,3,2,1,0:T(8,128)} %bitcast.68, f32[6,4,512,512]{3,2,1,0:T(8,128)} %kernel_ref.1, bf16[2,256,512]{2,1,0:T(8,128)(2,1)} %constant.71.clone.fy_ref, bf16[2,512,256]{2,1,0:T(8,128)(2,1)} %constant.72.clone.fx_ref, bf16[2,256,512]{2,1,0:T(8,128)(2,1)} %constant.73.clone.gx_ref, ...), custom_call_target="tpu_custom_call" | custom-call | flops 28991029248 | bytes 25165824 | tf_op jit(solution)/shard_map/plane_kernel/pallas_call | solution.py:469
  104.1 0.0 collective-permute-done.2
  104.1 0.0 collective-permute-done.3
  104.1 0.0 copy-done
  104.1 2.3 pad_maximum_fusion.1
  106.5 0.0 collective-permute-done
  106.5 0.0 collective-permute-done.1
  106.5 5.3 %pad_maximum_fusion = f32[4,3,8,64,256]{4,3,2,1,0:T(8,128)} fusion(f32[1,3,8,64,256]{4,3,2,1,0:T(8,128)} %collective-permute-done.1, f32[2,3,8,64,256]{4,3,2,1,0:T(8,128)S(1)} %copy-done, f32[1,3,8,64,256]{4,3,2,1,0:T(8,128)} %collective-permute-done), kind=kLoop, calls=%fused_computation.8 | loop fusion | flops 3145728 | bytes 12582912 | tf_op jit(solution)/shard_map/concatenate | solution.py:26
  111.8 10.6 %all-to-all-start = ((f32[16,3,2,64,256]{4,3,2,1,0:T(8,128)}), f32[16,3,2,64,256]{4,3,2,1,0:T(8,128)}, u32[]{:S(2)}, u32[]{:S(2)}) async-start(f32[16,3,2,64,256]{4,3,2,1,0:T(8,128)} %bitcast.67), calls=%async_computation | async-start | bytes 12582912 | tf_op jit(solution)/shard_map/all_to_all | solution.py:495
  122.3 2.0 copy.76
  124.4 0.0 copy-done.9
  124.4 0.1 compare_bitcast_fusion
  124.5 0.9 add_subtract_fusion
  125.5 5.4 %subtract_multiply_fusion = (f32[2,1,8,64,256]{4,3,2,1,0:T(8,128)}, f32[2,1,8,64,256]{4,3,2,1,0:T(8,128)}, f32[2,1,8,64,256]{4,3,2,1,0:T(8,128)}) fusion(f32[2,3,8,66,256]{4,3,2,1,0:T(8,128)} %pad_maximum_fusion.1, f32[2,3,8,64,256]{4,3,2,1,0:T(8,128)S(1)} %copy-done, f32[64]{0:T(128)S(1)} %broadcast_multiply_fusion), kind=kLoop, calls=%fused_computation.58 | loop fusion | flops 2621440 | bytes 11534848 | tf_op jit(solution)/shard_map/mul | solution.py:551
  130.8 0.0 copy-done.1
  130.8 10.6 %multiply_reduce_fusion.8 = (f32[2,8,64,256]{3,2,1,0:T(8,128)}, f32[2,8,64,256]{3,2,1,0:T(8,128)}, f32[2,8,64,256]{3,2,1,0:T(8,128)}, f32[2,8,64,256,3]{3,2,1,4,0:T(8,128)}, f32[2,3,8,64,256]{4,3,2,1,0:T(8,128)}) fusion(f32[2,3,8,64,256]{4,3,2,1,0:T(8,128)S(1)} %copy-done, f32[4,3,8,64,256]{4,3,2,1,0:T(8,128)} %pad_maximum_fusion, ...), kind=kLoop, calls=%fused_computation.34 | loop fusion | flops 14155776 | bytes 28835840 | tf_op jit(solution)/shard_map/reduce_sum | solution.py:46
  141.5 2.6 %fusion.15 = f32[1,2,8,64,256]{4,3,2,1,0:T(8,128)S(1)} fusion(f32[2,8,64,256,3]{3,2,1,4,0:T(8,128)} %get-tuple-element.44, f32[2,8,64,256,3]{3,2,1,0,4:T(8,128)} %bitcast.65), kind=kLoop, calls=%fused_computation.51 | loop fusion | flops 786432 | bytes 5242880 | tf_op jit(solution)/shard_map/jit(cross)/sub | solution.py:50
  144.1 0.5 copy-done.5
  144.6 2.8 %subtract_bitcast_fusion = (f32[1,2,8,64,256]{4,3,2,1,0:T(8,128)S(1)}, f32[1,2,8,64,256]{4,3,2,1,0:T(8,128)S(1)}) fusion(f32[2,8,64,256,3]{3,2,1,4,0:T(8,128)S(1)} %copy-done.5, f32[2,8,64,256,3]{3,2,1,0,4:T(8,128)} %bitcast.66), kind=kLoop, calls=%fused_computation.57 | loop fusion | flops 1572864 | bytes 8388608 | tf_op jit(solution)/shard_map/jit(cross)/sub | solution.py:50
  147.5 0.3 fusion.7
  147.8 0.9 copy-done.6
  148.7 1.9 multiply_reduce_fusion.12
  150.6 0.0 copy-done.7
  150.7 4.1 %multiply_reduce_fusion.4 = (f32[2]{0:T(128)S(1)}, f32[2]{0:T(128)S(1)}, f32[2]{0:T(128)S(1)}, f32[2,3,8,64,256]{4,3,2,1,0:T(8,128)}, f32[2,3,8,64,256]{4,3,2,1,0:T(8,128)}) fusion(f32[2,3,8,64,256]{4,3,2,1,0:T(8,128)S(1)} %copy-done, f32[2,8,64,256]{3,2,1,0:T(8,128)S(1)} %copy-done.7, f32[4,3,8,64,256]{4,3,2,1,0:T(8,128)S(1)} %bitcast.64, ...), kind=kLoop, calls=%fused_computation.27 | loop fusion | flops 9437178 | bytes 17825816 | tf_op jit(solution)/shard_map/reduce_sum | solution.py:42
  154.8 37.1 %all-to-all-done.in_ref = f32[16,3,2,64,256]{4,3,2,1,0:T(8,128)} async-done(((f32[16,3,2,64,256]{4,3,2,1,0:T(8,128)}), f32[16,3,2,64,256]{4,3,2,1,0:T(8,128)}, u32[]{:S(2)}, u32[]{:S(2)}) %all-to-all-start) | async-done | bytes 6291488 | tf_op jit(solution)/shard_map/all_to_all | solution.py:495
  191.8 6.0 %planes_to_layers.1 = f32[2,3,8,64,256]{4,3,2,1,0:T(8,128)} custom-call(f32[16,3,2,64,256]{4,3,2,1,0:T(8,128)} %all-to-all-done.in_ref), custom_call_target="tpu_custom_call" | custom-call | tf_op jit(solution)/shard_map/planes_to_layers/pallas_call | solution.py:498
  197.9 4.3 %multiply_reduce_fusion.10 = (f32[2]{0:T(128)S(1)}, f32[2,8,64,256]{3,2,1,0:T(8,128)S(1)}, f32[2,3,8,64,256]{4,3,2,1,0:T(8,128)S(1)}) fusion(f32[2,3,8,64,256]{4,3,2,1,0:T(8,128)S(1)} %copy-done, f32[2,3,8,64,256]{4,3,2,1,0:T(8,128)} %get-tuple-element.15, f32[2,3,8,64,256]{4,3,2,1,0:T(8,128)} %planes_to_layers.1), kind=kLoop, calls=%fused_computation.39 | loop fusion | flops 2883582 | bytes 13631496 | tf_op jit(solution)/shard_map/reduce_sum | solution.py:42
  202.2 0.0 copy-done.2
  202.2 0.4 copy-done.3
  202.6 3.1 %multiply_reduce_fusion.2 = (f32[2]{0:T(128)S(1)}, f32[2]{0:T(128)S(1)}, f32[2,3,8,64,256]{4,3,2,1,0:T(8,128)}) fusion(f32[2,3,8,64,256]{4,3,2,1,0:T(8,128)S(1)} %copy-done.3, f32[2,3,8,64,256]{4,3,2,1,0:T(8,128)S(1)} %copy-done.2, f32[2,3,8,64,256]{4,3,2,1,0:T(8,128)S(1)} %get-tuple-element.39, f32[2,3,8,64,256]{4,3,2,1,0:T(8,128)S(1)} %copy-done, ...), kind=kLoop, calls=%fused_computation.24 | loop fusion | flops 4718588 | bytes 16777232 | tf_op jit(solution)/shard_map/reduce_sum | solution.py:42
  205.7 0.1 copy.71
  205.8 0.1 copy.72
  205.9 0.1 copy.66
  206.0 0.1 copy.67
  206.1 0.1 copy.68
  206.2 0.1 copy.69
  206.3 0.1 copy.70
  206.4 0.1 stack.39
  206.5 0.6 pad.13.tile_ref
  207.1 11.5 %swap_kernel.2 = f32[3,8,128]{2,1,0:T(8,128)} custom-call(f32[8,128]{1,0:T(8,128)} %pad.13.tile_ref), custom_call_target="tpu_custom_call" | custom-call | tf_op jit(solution)/shard_map/swap_kernel/pallas_call | solution.py:421
  218.6 0.7 slice_bitcast_fusion.5
  219.2 0.7 slice_bitcast_fusion.3
  220.0 0.6 multiply_reduce_fusion.13
  220.6 0.1 select_select_fusion.1
  220.7 0.6 slice.229
  221.3 0.8 fusion.23
  222.1 0.1 slice_reduce_fusion
  222.2 0.1 slice_reduce_fusion.1
  222.3 7.0 %multiply_reduce_fusion.1 = (f32[2,8,64,256]{3,2,1,0:T(8,128)S(1)}, f32[2,3,8,64,256]{4,3,2,1,0:T(8,128)}) fusion(f32[2,3,8,64,256]{4,3,2,1,0:T(8,128)} %get-tuple-element.41, f32[2]{0:T(128)S(1)} %slice_reduce_fusion, f32[2,3,8,64,256]{4,3,2,1,0:T(8,128)} %get-tuple-element.38, f32[2,3,8,64,256]{4,3,2,1,0:T(8,128)} %get-tuple-element.40, ...), kind=kLoop, calls=%fused_computation.22 | loop fusion | flops 5242880 | bytes 13631506 | tf_op jit(solution)/shard_map/reduce_sum | solution.py:620
  229.3 0.4 sqrt_reduce_fusion
  229.7 0.6 pad.14.tile_ref
  230.3 5.0 %swap_kernel.3 = f32[1,8,128]{2,1,0:T(8,128)} custom-call(f32[8,128]{1,0:T(8,128)} %pad.14.tile_ref), custom_call_target="tpu_custom_call" | custom-call | tf_op jit(solution)/shard_map/swap_kernel/pallas_call | solution.py:421
  235.3 0.7 minimum_bitcast_fusion
  236.0 3.0 %multiply_reduce_fusion = f32[2,8,64,256]{3,2,1,0:T(8,128)S(1)} fusion(f32[2,3,8,64,256]{4,3,2,1,0:T(8,128)S(1)} %copy-done, f32[2,3,8,64,256]{4,3,2,1,0:T(8,128)} %get-tuple-element.32, f32[2]{0:T(128)S(1)} %minimum_bitcast_fusion), kind=kLoop, calls=%fused_computation.20 | loop fusion | flops 2883584 | bytes 7340040 | tf_op jit(solution)/shard_map/reduce_sum | solution.py:624
  238.9 0.2 sqrt.29
  239.2 0.0 copy-done.4
  239.2 2.5 %broadcast_divide_fusion = f32[2,3,8,64,256]{4,3,2,1,0:T(8,128)} fusion(f32[2,8,64,256]{3,2,1,0:T(8,128)S(1)} %sqrt.29, f32[2,3,8,64,256]{4,3,2,1,0:T(8,128)S(1)} %copy-done, f32[2,3,8,64,256]{4,3,2,1,0:T(8,128)S(1)} %copy-done.4, f32[2]{0:T(128)S(1)} %minimum_bitcast_fusion), kind=kLoop, calls=%fused_computation.38 | loop fusion | flops 2359296 | bytes 10485768 | tf_op jit(solution)/shard_map/div | solution.py:624
  (25 shorter events, 0.1 us)
Async XLA Ops:
  4.5 101.9 %collective-permute-start = (f32[1,3,8,64,256]{4,3,2,1,0:T(8,128)}, f32[1,3,8,64,256]{4,3,2,1,0:T(8,128)}, u32[]{:S(2)}, u32[]{:S(2)}) collective-permute-start(f32[1,3,8,64,256]{4,3,2,1,0:T(8,128)} %get-tuple-element.51), channel_id=1, source_target_pairs={{0,4},{4,8},{8,12},{12,16},{16,20},{20,24},{24,28},{1,5},{5,9},{9,... | collective-permute-start | bytes 4718600 | tf_op jit(solution)/shard_map/ppermute | solution.py:28
  10.6 95.9 %collective-permute-start.1 = (f32[1,3,8,64,256]{4,3,2,1,0:T(8,128)}, f32[1,3,8,64,256]{4,3,2,1,0:T(8,128)}, u32[]{:S(2)}, u32[]{:S(2)}) collective-permute-start(f32[1,3,8,64,256]{4,3,2,1,0:T(8,128)} %get-tuple-element.52), channel_id=1, source_target_pairs={{4,0},{8,4},{12,8},{16,12},{20,16},{24,20},{28,24},{5,1},{9,5},{13... | collective-permute-start | bytes 4718600 | tf_op jit(solution)/shard_map/ppermute | solution.py:30
  13.1 91.0 %collective-permute-start.2 = (f32[2,3,8,1,256]{4,3,2,1,0:T(1,128)S(1)}, f32[2,3,8,1,256]{4,3,2,1,0:T(1,128)S(1)}, u32[]{:S(2)}, u32[]{:S(2)}) collective-permute-start(f32[2,3,8,1,256]{4,3,2,1,0:T(1,128)S(1)} %get-tuple-element.49), channel_id=1, source_target_pairs={{0,1},{1,2},{2,3},{4,5},{5,6},{6,7},{8,9},{9,10},{10,11},{12,13},{... | collective-permute-start | bytes 147464 | tf_op jit(solution)/shard_map/ppermute | solution.py:28
  14.6 89.5 %collective-permute-start.3 = (f32[2,3,8,1,256]{4,3,2,1,0:T(1,128)S(1)}, f32[2,3,8,1,256]{4,3,2,1,0:T(1,128)S(1)}, u32[]{:S(2)}, u32[]{:S(2)}) collective-permute-start(f32[2,3,8,1,256]{4,3,2,1,0:T(1,128)S(1)} %get-tuple-element.50), channel_id=1, source_target_pairs={{1,0},{2,1},{3,2},{5,4},{6,5},{7,6},{9,8},{10,9},{11,10},{13,12},{... | collective-permute-start | bytes 147464 | tf_op jit(solution)/shard_map/ppermute | solution.py:30
  21.4 82.7 %copy-start = (f32[2,3,8,64,256]{4,3,2,1,0:T(8,128)S(1)}, f32[2,3,8,64,256]{4,3,2,1,0:T(8,128)}, u32[]{:S(2)}) copy-start(f32[2,3,8,64,256]{4,3,2,1,0:T(8,128)} %in_ref.1) | copy-start | bytes 9437188
  111.8 80.1 %all-to-all-start = ((f32[16,3,2,64,256]{4,3,2,1,0:T(8,128)}), f32[16,3,2,64,256]{4,3,2,1,0:T(8,128)}, u32[]{:S(2)}, u32[]{:S(2)}) async-start(f32[16,3,2,64,256]{4,3,2,1,0:T(8,128)} %bitcast.67), calls=%async_computation | async-start | bytes 12582912 | tf_op jit(solution)/shard_map/all_to_all | solution.py:495
  122.3 2.1 copy-start.9
  125.5 5.4 %copy-start.1 = (f32[2,3,8,66,256]{4,3,2,1,0:T(8,128)S(1)}, f32[2,3,8,66,256]{4,3,2,1,0:T(8,128)}, u32[]{:S(2)}) copy-start(f32[2,3,8,66,256]{4,3,2,1,0:T(8,128)} %pad_maximum_fusion.1) | copy-start | bytes 9732100
  141.5 3.2 %copy-start.5 = (f32[2,8,64,256,3]{3,2,1,4,0:T(8,128)S(1)}, f32[2,8,64,256,3]{3,2,1,4,0:T(8,128)}, u32[]{:S(2)}) copy-start(f32[2,8,64,256,3]{3,2,1,4,0:T(8,128)} %get-tuple-element.44) | copy-start | bytes 9437188
  141.5 9.2 %slice-start = ((s8[6291456]{0:T(1024)(128)(4,1)}), s8[4194304]{0:T(1024)(128)(4,1)S(1)}, s32[]{:S(2)}) async-start(s8[6291456]{0:T(1024)(128)(4,1)} %bitcast.63), calls=%async_computation.1 | async-start | bytes 8388608
  144.6 6.0 %slice-start.1 = ((s8[6291456]{0:T(1024)(128)(4,1)}), s8[2097152]{0:T(1024)(128)(4,1)S(1)}, s32[]{:S(2)}) async-start(s8[6291456]{0:T(1024)(128)(4,1)} %bitcast.63), calls=%async_computation.2 | async-start | bytes 4194304
  147.5 1.2 copy-start.6
  147.5 3.2 %copy-start.7 = (f32[2,8,64,256]{3,2,1,0:T(8,128)S(1)}, f32[2,8,64,256]{3,2,1,0:T(8,128)}, u32[]{:S(2)}) copy-start(f32[2,8,64,256]{3,2,1,0:T(8,128)} %get-tuple-element.21) | copy-start | bytes 3145732
  147.5 3.2 %copy-start.8 = (f32[2,8,64,256]{3,2,1,0:T(8,128)S(1)}, f32[2,8,64,256]{3,2,1,0:T(8,128)}, u32[]{:S(2)}) copy-start(f32[2,8,64,256]{3,2,1,0:T(8,128)} %get-tuple-element.22) | copy-start | bytes 3145732
  197.9 4.3 %copy-start.2 = (f32[2,3,8,64,256]{4,3,2,1,0:T(8,128)S(1)}, f32[2,3,8,64,256]{4,3,2,1,0:T(8,128)}, u32[]{:S(2)}) copy-start(f32[2,3,8,64,256]{4,3,2,1,0:T(8,128)} %get-tuple-element.40) | copy-start | bytes 9437188
  197.9 4.7 %copy-start.3 = (f32[2,3,8,64,256]{4,3,2,1,0:T(8,128)S(1)}, f32[2,3,8,64,256]{4,3,2,1,0:T(8,128)}, u32[]{:S(2)}) copy-start(f32[2,3,8,64,256]{4,3,2,1,0:T(8,128)} %get-tuple-element.41) | copy-start | bytes 9437188
  236.0 3.2 %copy-start.4 = (f32[2,3,8,64,256]{4,3,2,1,0:T(8,128)S(1)}, f32[2,3,8,64,256]{4,3,2,1,0:T(8,128)}, u32[]{:S(2)}) copy-start(f32[2,3,8,64,256]{4,3,2,1,0:T(8,128)} %get-tuple-element.32) | copy-start | bytes 9437188
